TPU v7x, 32 devices: a whole 2x2x4 slice. The times are simulated.
32 devices in a mesh: rep: 16 (over z, x, core), tp: 2 (over y).
Axes of the slice: x: 2, y: 2, z: 4, core: 2. Of those that a mesh axis runs over, the one named last changes fastest.
Arguments:
- tokens: bfloat16 [16, 256, 3072], P('rep', 'tp'), may hold values from -100 to 100
- norm_gain: float32 [16, 3072], P('rep'), may hold values from 0.5 to 1.5
- w_query: bfloat16 [16, 3072, 2048], P('rep', None, 'tp'), may hold values from -1 to 1
- key_weight: bfloat16 [16, 3072, 1024], P('rep', None, 'tp'), may hold values from -1 to 1
- value_weight: bfloat16 [16, 3072, 1024], P('rep', None, 'tp'), may hold values from -0.109375 to 0.109375
- attention_gradient: bfloat16 [16, 256, 2048], P('rep', None, 'tp'), may hold values from -6 to 6
- global_fragment: float32 [128, 3072], P('tp'), may hold values from -6 to 6
- momentum: float32 [128, 3072], P('tp'), may hold values from -3 to 3
- local_fragment: bfloat16 [16, 128, 3072], P('rep', 'tp'), may hold values from -6 to 6
Outputs:
- grad_query_w: bfloat16 [16, 3072, 2048], P('rep', None, 'tp')
- grad_key_w: bfloat16 [16, 3072, 1024], P('rep', None, 'tp')
- grad_value_w: bfloat16 [16, 3072, 1024], P('rep', None, 'tp')
- grad_gain: float32 [16, 3072], P('rep')
- grad_tokens: bfloat16 [16, 256, 3072], P('rep', 'tp')
- new_global: float32 [128, 3072], P('tp')
- new_momentum: float32 [128, 3072], P('tp')
All inputs are finite; a program needn't handle non-finite values.
Results may differ from a plain program's by a relative error of at most 0.019.
The roundings to bfloat16 on the way count: a program that leaves them out, or rounds other values in their place, can miss the bound.
Values may be sent and summed in bfloat16 or wider, within the bound.
A program may use at most 128 MiB of HBM per device.

v0:
```python
import jax
import jax.numpy as jnp
from jax import lax
from jax.sharding import PartitionSpec as P

HEAD_SIZE = 128


epsilon = 1e-05
rope_base = 500000.0
outer_rate = 0.7
outer_momentum = 0.9


def rope_tables(sequence_length, width):
    middle = width // 2
    frequency = rope_base ** (-2.0 * jnp.arange(middle, dtype=jnp.float32) / width)
    angles = jnp.arange(sequence_length, dtype=jnp.float32)[:, None] * frequency[None, :]
    angles = jnp.concatenate([angles, angles], axis=1)
    return (jnp.cos(angles)[:, None, :], jnp.sin(angles)[:, None, :])


def rotate(vectors, cosine_table, sine_table):
    middle = vectors.shape[-1] // 2
    turned = jnp.concatenate([-vectors[..., middle:], vectors[..., :middle]], axis=-1)
    return vectors * cosine_table + turned * sine_table


def reverse_rotation(gradient, cosine_table, sine_table):
    middle = gradient.shape[-1] // 2
    shifted = gradient * sine_table
    turned = jnp.concatenate([shifted[..., middle:], -shifted[..., :middle]], axis=-1)
    return gradient * cosine_table + turned


def attention_reverse(query_rows, rotated_keys, values_bfloat, grad_out, block_of_rows):
    sequence_length = query_rows.shape[0]
    score_scale = query_rows.shape[-1] ** (-0.5)

    def one_block(running, block_index):
        acc_key, acc_value = running
        offset = block_index * block_of_rows
        query_block = lax.dynamic_slice_in_dim(query_rows, offset, block_of_rows, 0)
        grad_block = lax.dynamic_slice_in_dim(grad_out, offset, block_of_rows, 0)
        scores = (
            jnp.einsum(
                "qgrd,kgd->grqk", query_block, rotated_keys, preferred_element_type=jnp.float32
            )
            * score_scale
        )
        row_pos = offset + jnp.arange(block_of_rows)
        col_pos = jnp.arange(sequence_length)
        allowed = col_pos[None, :] <= row_pos[:, None]
        scores = jnp.where(allowed, scores, -jnp.inf)
        highest = jnp.max(scores, axis=-1, keepdims=True)
        powers = jnp.exp(scores - highest)
        probability = powers / jnp.sum(powers, axis=-1, keepdims=True)
        prob_low = probability.astype(jnp.bfloat16)
        acc_value = acc_value + jnp.einsum(
            "grqk,qgrd->kgd", prob_low, grad_block, preferred_element_type=jnp.float32
        )
        grad_prob = jnp.einsum(
            "qgrd,kgd->grqk", grad_block, values_bfloat, preferred_element_type=jnp.float32
        )
        grad_score = (
            probability
            * (grad_prob - jnp.sum(grad_prob * probability, axis=-1, keepdims=True))
            * score_scale
        )
        score_low = grad_score.astype(jnp.bfloat16)
        grad_query = jnp.einsum(
            "grqk,kgd->qgrd", score_low, rotated_keys, preferred_element_type=jnp.float32
        )
        acc_key = acc_key + jnp.einsum(
            "grqk,qgrd->kgd", score_low, query_block, preferred_element_type=jnp.float32
        )
        return ((acc_key, acc_value), grad_query)

    initial = jnp.zeros(rotated_keys.shape, jnp.float32)
    (acc_key, acc_value), grad_blocks = lax.scan(
        one_block, (initial, initial), jnp.arange(sequence_length // block_of_rows)
    )
    return (grad_blocks.reshape(query_rows.shape), acc_key, acc_value)


def body(
    tokens,
    norm_gain,
    w_query,
    key_weight,
    value_weight,
    attention_gradient,
    global_fragment,
    momentum,
    local_fragment,
):
    local_rows = tokens[0]
    norm_gains = norm_gain[0]
    weight_q = w_query[0]
    weight_k = key_weight[0]
    weight_v = value_weight[0]
    widened_rows = local_rows.astype(jnp.float32)
    inverse_norm = lax.rsqrt(
        jnp.mean(widened_rows * widened_rows, axis=-1, keepdims=True) + epsilon
    )
    normalized_input = widened_rows * inverse_norm
    normalized_local = (normalized_input * norm_gains[None, :]).astype(jnp.bfloat16)
    normalized = lax.all_gather(normalized_local, "tp", axis=0, tiled=True)
    sequence_length = normalized.shape[0]
    heads_q = weight_q.shape[1] // HEAD_SIZE
    heads_kv = weight_k.shape[1] // HEAD_SIZE
    cosine_table, sine_table = rope_tables(sequence_length, HEAD_SIZE)
    query_rows = jnp.dot(normalized, weight_q, preferred_element_type=jnp.float32).reshape(
        sequence_length, heads_q, HEAD_SIZE
    )
    query_rows = rotate(query_rows, cosine_table, sine_table).astype(jnp.bfloat16)
    rotated_keys = jnp.dot(normalized, weight_k, preferred_element_type=jnp.float32).reshape(
        sequence_length, heads_kv, HEAD_SIZE
    )
    rotated_keys = rotate(rotated_keys, cosine_table, sine_table).astype(jnp.bfloat16)
    values_bfloat = (
        jnp.dot(normalized, weight_v, preferred_element_type=jnp.float32)
        .astype(jnp.bfloat16)
        .reshape(sequence_length, heads_kv, HEAD_SIZE)
    )
    replica_group = heads_q // heads_kv
    block_of_rows = min(512, sequence_length)
    query_input_gradient, key_input_gradient, value_input_gradient = attention_reverse(
        query_rows.reshape(sequence_length, heads_kv, replica_group, HEAD_SIZE),
        rotated_keys,
        values_bfloat,
        attention_gradient[0].reshape(sequence_length, heads_kv, replica_group, HEAD_SIZE),
        block_of_rows,
    )
    dquery = (
        reverse_rotation(
            query_input_gradient.reshape(sequence_length, heads_q, HEAD_SIZE),
            cosine_table,
            sine_table,
        )
        .astype(jnp.bfloat16)
        .reshape(sequence_length, heads_q * HEAD_SIZE)
    )
    key_gradient = (
        reverse_rotation(key_input_gradient, cosine_table, sine_table)
        .astype(jnp.bfloat16)
        .reshape(sequence_length, heads_kv * HEAD_SIZE)
    )
    value_gradient = value_input_gradient.astype(jnp.bfloat16).reshape(
        sequence_length, heads_kv * HEAD_SIZE
    )
    contract = (((0,), (0,)), ((), ()))
    grad_wq = lax.dot_general(
        normalized, dquery, contract, preferred_element_type=jnp.float32
    ).astype(jnp.bfloat16)
    grad_wk = lax.dot_general(
        normalized, key_gradient, contract, preferred_element_type=jnp.float32
    ).astype(jnp.bfloat16)
    grad_wv = lax.dot_general(
        normalized, value_gradient, contract, preferred_element_type=jnp.float32
    ).astype(jnp.bfloat16)
    back = (((1,), (1,)), ((), ()))
    partial_value = lax.dot_general(dquery, weight_q, back, preferred_element_type=jnp.float32)
    partial_value = partial_value + lax.dot_general(
        key_gradient, weight_k, back, preferred_element_type=jnp.float32
    )
    summed_rows = lax.psum_scatter(
        (
            partial_value
            + lax.dot_general(value_gradient, weight_v, back, preferred_element_type=jnp.float32)
        ).astype(jnp.bfloat16),
        "tp",
        scatter_dimension=0,
        tiled=True,
    ).astype(jnp.float32)
    gains_gradient = lax.psum(jnp.sum(summed_rows * normalized_input, axis=0), "tp")
    scaled_rows = summed_rows * norm_gains[None, :]
    gradient_rows = (
        inverse_norm
        * (
            scaled_rows
            - normalized_input * jnp.mean(scaled_rows * normalized_input, axis=-1, keepdims=True)
        )
    ).astype(jnp.bfloat16)
    delta = global_fragment - local_fragment[0].astype(jnp.float32)
    replicas = lax.axis_size("rep")
    mean_delta = lax.psum(delta, "rep") / replicas
    new_momentum = outer_momentum * momentum + mean_delta
    new_global = global_fragment - outer_rate * (mean_delta + outer_momentum * new_momentum)
    return (
        grad_wq[None],
        grad_wk[None],
        grad_wv[None],
        gains_gradient[None],
        gradient_rows[None],
        new_global,
        new_momentum,
    )


def solution(mesh):
    placed = (
        P("rep", "tp", None),
        P("rep", None),
        P("rep", None, "tp"),
        P("rep", None, "tp"),
        P("rep", None, "tp"),
        P("rep", None, "tp"),
        P("tp", None),
        P("tp", None),
        P("rep", "tp", None),
    )
    return jax.shard_map(
        body,
        mesh=mesh,
        in_specs=placed,
        out_specs=(
            P("rep", None, "tp"),
            P("rep", None, "tp"),
            P("rep", None, "tp"),
            P("rep", None),
            P("rep", "tp", None),
            P("tp", None),
            P("tp", None),
        ),
        check_vma=False,
    )
```

profile of v0, /device:TPU:0, one launch (start us, length us, event | category | flops | bytes accessed | tf_op | source)
XLA Modules:
  0.0 146.9 jit_solution(9005998716346742518)
XLA Ops:
  8.0 0.0 all-gather.2.cloned.1.call-start
  8.1 1.6 %fusion.25 = f32[128]{0:T(128)S(1)} fusion(bf16[1,128,3072]{2,1,0:T(8,128)(2,1)} %param.9), kind=kLoop, calls=%fused_computation.37 | loop fusion | flops 1179520 | bytes 786944 | tf_op jit(solution)/shard_map/reduce_sum | solution.py:104
  9.6 2.3 %fusion.22 = bf16[128,3072]{1,0:T(8,128)(2,1)} fusion(bf16[1,128,3072]{2,1,0:T(8,128)(2,1)} %param.9, f32[3072]{0:T(1024)} %bitcast.153, f32[128]{0:T(128)S(1)} %add_rsqrt_fusion), kind=kLoop, calls=%fused_computation.34 | loop fusion | flops 1572864 | bytes 1585664 | tf_op jit(solution)/shard_map/convert_element_type | solution.py:107
  11.9 0.0 all-gather.2.cloned.1.call-update
  11.9 0.0 all-reduce.2.cloned.1.call-start
  12.0 2.1 %convert_subtract_fusion = f32[64,3072]{1,0:T(8,128)} fusion(f32[64,3072]{1,0:T(8,128)} %param.15, bf16[1,64,3072]{2,1,0:T(8,128)(2,1)S(1)} %copy-done.19), kind=kLoop, calls=%fused_computation.65 | loop fusion | flops 393216 | bytes 1966080 | tf_op jit(solution)/shard_map/sub | solution.py:185
  14.1 0.0 all-reduce.2.cloned.1.call-update
  14.1 0.0 reduce-scatter.2.cloned.1.call-start
  14.2 8.7 %copy.38 = bf16[1024,3072]{1,0:T(8,128)(2,1)} copy(bf16[1024,3072]{0,1:T(8,128)(2,1)} %bitcast.138) | data formatting | bytes 12582912 | tf_op jit(solution)/shard_map/dot_general | solution.py:113
  22.9 0.1 iota_multiply_fusion
  23.0 0.5 fusion.56
  23.4 4.7 %copy.35 = bf16[512,3072]{1,0:T(8,128)(2,1)} copy(bf16[512,3072]{0,1:T(8,128)(2,1)} %bitcast.137) | data formatting | bytes 6291456 | tf_op jit(solution)/shard_map/dot_general | solution.py:117
  28.1 2.0 %copy.41 = bf16[1,256,1024]{1,2,0:T(8,128)(2,1)} copy(bf16[1,256,1024]{2,1,0:T(8,128)(2,1)} %param.14) | data formatting | bytes 1048576 | tf_op jit(solution)/shard_map/reshape;squeeze | solution.py:132
  30.2 11.8 %all-gather.2.cloned.1.call-done = bf16[256,3072]{1,0:T(8,128)(2,1)} async-done(((bf16[128,3072]{1,0:T(8,128)(2,1)}), bf16[256,3072]{1,0:T(8,128)(2,1)}) %all-gather.2.cloned.1.call-update) | async-done | bytes 1572880 | tf_op jit(solution)/shard_map/all_gather | solution.py:108
  42.0 5.3 %fusion.26 = f32[256,8,128]{0,2,1:T(8,128)S(1)} fusion(bf16[8,128,3072]{2,1,0:T(8,128)(2,1)} %bitcast.141, bf16[256,3072]{1,0:T(8,128)(2,1)} %all-gather.2.cloned.1.call-done), kind=kOutput, calls=%fused_computation.38 | convolution fusion | flops 1610612736 | bytes 8912896 | tf_op jit(solution)/shard_map/dot_general | solution.py:113
  47.3 1.1 slice_negate_fusion.1
  48.4 1.1 copy-done.1
  49.5 1.1 fusion.28
  50.5 0.9 slice_negate_fusion.3
  51.5 0.0 copy-done.9
  51.5 1.7 %fusion.30 = bf16[256,512]{1,0:T(8,128)(2,1)} fusion(bf16[256,3072]{1,0:T(8,128)(2,1)S(1)} %copy-done.1, bf16[1,3072,512]{2,1,0:T(8,128)(2,1)S(1)} %copy-done), kind=kOutput, calls=%fused_computation.44 | convolution fusion | flops 805437440 | bytes 4980736 | tf_op jit(solution)/shard_map/dot_general | solution.py:122
  53.2 1.7 %reshape.115 = bf16[256,4,128]{2,1,0:T(4,128)(2,1)} reshape(bf16[256,512]{1,0:T(8,128)(2,1)} %fusion.30) | data formatting | bytes 524288 | tf_op jit(solution)/shard_map/reshape | solution.py:124
  55.0 2.7 %fusion.35 = bf16[256,8,128]{0,2,1:T(8,128)(2,1)} fusion(f32[256,8,64]{0,2,1:T(8,128)} %get-tuple-element.40, f32[256,8,64]{0,2,1:T(8,128)} %get-tuple-element.39, f32[256,8,128]{0,2,1:T(8,128)} %copy-done.7, f32[256,128]{0,1:T(8,128)S(1)} %get-tuple-element.46, f32[256,128]{0,1:T(8,128)S(1)} %get-tuple-element.45), kind=kLoop, calls=%fused_computation.48 | loop fusion | flops 1310720 | bytes 2883584 | tf_op jit(solution)/shard_map/convert_element_type | solution.py:116
  57.7 0.8 fusion.50
  58.5 1.7 %fusion.51 = f32[4,256,256,2]{2,1,3,0:T(8,128)} fusion(bf16[256,4,2,128]{0,3,2,1:T(8,128)(2,1)S(1)} %bitcast.146, bf16[256,4,128,1]{2,1,0,3:T(4,128)(2,1)S(1)} %bitcast.149), kind=kOutput, calls=%fused_computation.78 | convolution fusion | flops 134217728 | bytes 2883584 | tf_op jit(solution)/shard_map/while/body/eval_jaxpr/qgrd,kgd->grqk/dot_general | solution.py:62
  60.2 3.3 %fusion.65 = (f32[4,2,256]{2,1,0:T(2,128)S(1)}, f32[4,2,256,256]{2,3,1,0:T(8,128)}) fusion(pred[256,256]{0,1:T(8,128)(4,1)S(1)} %iota_compare_fusion, bf16[256,4,128,1]{0,2,3,1:T(8,128)(2,1)} %fusion.50, bf16[256,4,2,128]{0,3,2,1:T(8,128)(2,1)} %bitcast.150), kind=kOutput, calls=%fused_computation.98 | convolution fusion | flops 136315136 | bytes 2957312 | tf_op jit(solution)/shard_map/while/body/eval_jaxpr/sub | solution.py:56
  63.5 5.4 %broadcast_multiply_fusion = (f32[256,4,128]{0,2,1:T(8,128)}, f32[256,4,128]{0,2,1:T(8,128)}) fusion(f32[256,128]{0,1:T(8,128)S(1)} %get-tuple-element.46, bf16[256,4,2,128]{0,3,2,1:T(8,128)(2,1)} %bitcast.151, f32[4,256,256,2]{2,1,3,0:T(8,128)} %fusion.51, f32[4,2,256,256]{2,3,1,0:T(8,128)} %get-tuple-element.48, f32[4,2,256]{2,1,0:T(2,128)S(1)} %get-tuple-element.47), kind=kOutput, calls=%fused_computation.81 | convolution fusion | flops 138021120 | bytes 5906432 | tf_op jit(solution)/shard_map/while/body/eval_jaxpr/grqk,qgrd->kgd/dot_general | solution.py:74
  68.8 5.3 %fusion.44 = f32[4,128,2,256]{3,1,2,0:T(8,128)} fusion(bf16[256,4,128,1]{0,2,3,1:T(8,128)(2,1)} %fusion.50, f32[4,256,256,2]{2,1,3,0:T(8,128)} %fusion.51, f32[4,2,256,256]{2,3,1,0:T(8,128)} %get-tuple-element.48, f32[4,2,256]{2,1,0:T(2,128)S(1)} %get-tuple-element.47), kind=kOutput, calls=%fused_computation.62 | convolution fusion | flops 137890048 | bytes 5513216 | tf_op jit(solution)/shard_map/while/body/eval_jaxpr/grqk,kgd->qgrd/dot_general | solution.py:71
  74.2 2.3 %fusion.33 = bf16[4,256,128]{1,2,0:T(8,128)(2,1)S(1)} fusion(bf16[256,4,2,128]{0,3,2,1:T(8,128)(2,1)} %bitcast.145, f32[4,2,256,256]{2,3,1,0:T(8,128)} %get-tuple-element.48, f32[4,2,256]{2,1,0:T(2,128)S(1)} %get-tuple-element.47), kind=kOutput, calls=%fused_computation.45 | convolution fusion | flops 135397376 | bytes 2891776 | tf_op jit(solution)/shard_map/while/body/eval_jaxpr/grqk,qgrd->kgd/dot_general | solution.py:59
  76.6 0.1 bitcast_multiply_fusion.3
  76.7 0.1 fusion.63
  76.7 1.1 fusion.39
  77.9 1.1 slice-done.1
  79.0 1.8 %fusion.2 = f32[256,3072]{1,0:T(8,128)S(1)} fusion(bf16[256,1024]{0,1:T(8,128)(2,1)S(1)} %bitcast.152, bf16[1,3072,1024]{2,1,0:T(8,128)(2,1)S(1)} %bitcast.140), kind=kOutput, calls=%fused_computation.2 | convolution fusion | flops 1610612736 | bytes 9961472 | tf_op jit(solution)/shard_map/dot_general | solution.py:163
  80.8 0.1 fusion.49
  80.9 0.1 copy-done.3
  81.0 1.1 convolution_add_fusion.1
  82.1 2.2 %fusion.6 = bf16[256,3072]{1,0:T(8,128)(2,1)} fusion(f32[256,3072]{1,0:T(8,128)S(1)} %convolution_add_fusion.1, bf16[256,512]{0,1:T(8,128)(2,1)S(1)} %bitcast.147, bf16[1,3072,512]{2,1,0:T(8,128)(2,1)S(1)} %copy-done), kind=kOutput, calls=%fused_computation.11 | convolution fusion | flops 806879232 | bytes 8126464 | tf_op jit(solution)/shard_map/dot_general | solution.py:170
  84.3 27.0 %all-reduce.2.cloned.1.call-done = f32[64,3072]{1,0:T(8,128)} async-done(((f32[64,3072]{1,0:T(8,128)}), f32[64,3072]{1,0:T(8,128)}) %all-reduce.2.cloned.1.call-update) | async-done | bytes 786448 | tf_op jit(solution)/shard_map/psum | solution.py:187
  111.3 3.1 %multiply_subtract_fusion = (f32[64,3072]{1,0:T(8,128)}, f32[64,3072]{1,0:T(8,128)}) fusion(f32[64,3072]{1,0:T(8,128)} %param.15, f32[64,3072]{1,0:T(8,128)} %all-reduce.2.cloned.1.call-done, f32[64,3072]{1,0:T(8,128)} %param.16), kind=kLoop, calls=%fused_computation.66 | loop fusion | flops 1376256 | bytes 3932160 | tf_op jit(solution)/shard_map/sub | solution.py:189
  114.5 0.2 fusion.37
  114.7 1.2 copy-done.2
  115.9 2.9 %fusion.5 = bf16[1,3072,512]{2,1,0:T(8,128)(2,1)} fusion(bf16[256,3072]{1,0:T(8,128)(2,1)S(1)} %copy-done.2, bf16[256,512]{0,1:T(8,128)(2,1)S(1)} %bitcast.148), kind=kOutput, calls=%fused_computation.8 | convolution fusion | flops 806879232 | bytes 4980736 | tf_op jit(solution)/shard_map/dot_general | solution.py:159
  118.8 2.7 %fusion.4 = bf16[1,3072,512]{2,1,0:T(8,128)(2,1)} fusion(bf16[256,3072]{1,0:T(8,128)(2,1)S(1)} %copy-done.2, bf16[256,512]{0,1:T(8,128)(2,1)S(1)} %bitcast.144), kind=kOutput, calls=%fused_computation.7 | convolution fusion | flops 806879232 | bytes 4980736 | tf_op jit(solution)/shard_map/dot_general | solution.py:156
  121.5 4.6 %convert_bitcast_fusion = bf16[1,3072,1024]{2,1,0:T(8,128)(2,1)} fusion(bf16[256,3072]{1,0:T(8,128)(2,1)S(1)} %copy-done.2, bf16[256,1024]{0,1:T(8,128)(2,1)S(1)} %fusion.37), kind=kOutput, calls=%fused_computation.4 | convolution fusion | flops 1613758464 | bytes 8388608 | tf_op jit(solution)/shard_map/dot_general | solution.py:153
  126.1 1.9 %fusion.24 = (f32[128]{0:T(128)S(1)}, f32[3072]{0:T(1024)S(1)}) fusion(bf16[128,3072]{1,0:T(8,128)(2,1)} %reduce-scatter.2.cloned.1.call-done, bf16[1,128,3072]{2,1,0:T(8,128)(2,1)} %param.9, f32[3072]{0:T(1024)S(1)} %bitcast.154, f32[128]{0:T(128)S(1)} %add_rsqrt_fusion), kind=kLoop, calls=%fused_computation.36 | loop fusion | flops 3142528 | bytes 1598464 | tf_op jit(solution)/shard_map/reduce_sum | solution.py:182
  128.0 8.8 %psum.14 = f32[1,3072]{1,0:T(1,128)} all-reduce(f32[1,3072]{1,0:T(1,128)S(1)} %bitcast.156), channel_id=1, replica_groups=mesh['rep'=16,'tp'=2] {'tp'}, use_global_device_ids=true, to_apply=%region_6.7 | all-reduce | flops 3072 | bytes 24576 | tf_op jit(solution)/shard_map/psum | solution.py:176
  136.8 2.7 %fusion.46 = bf16[1,128,3072]{2,1,0:T(8,128)(2,1)} fusion(bf16[128,3072]{1,0:T(8,128)(2,1)} %reduce-scatter.2.cloned.1.call-done, bf16[1,128,3072]{2,1,0:T(8,128)(2,1)} %param.9, f32[128]{0:T(128)S(1)} %broadcast_multiply_fusion.1, f32[3072]{0:T(1024)S(1)} %bitcast.155, f32[128]{0:T(128)S(1)} %add_rsqrt_fusion), kind=kLoop, calls=%fused_computation.64 | loop fusion | flops 3145728 | bytes 2372608 | tf_op jit(solution)/shard_map/broadcast_in_dim | solution.py:195
  (49 shorter events, 0.2 us)
Async XLA Ops:
  8.0 43.5 %copy-start = (bf16[1,3072,512]{2,1,0:T(8,128)(2,1)S(1)}, bf16[1,3072,512]{2,1,0:T(8,128)(2,1)}, u32[]{:S(2)}) copy-start(bf16[1,3072,512]{2,1,0:T(8,128)(2,1)} %param.13) | copy-start | bytes 9437188
  8.0 4.0 %copy-start.19 = (bf16[1,64,3072]{2,1,0:T(8,128)(2,1)S(1)}, bf16[1,64,3072]{2,1,0:T(8,128)(2,1)}, u32[]{:S(2)}) copy-start(bf16[1,64,3072]{2,1,0:T(8,128)(2,1)} %param.17) | copy-start | bytes 1179652
  8.0 34.0 %all-gather.2.cloned.1.call-start = ((), (), s32[]{:S(2)}) async-start(), calls=%async_computation.1 | async-start | bytes 2359296 | tf_op jit(solution)/shard_map/all_gather | solution.py:108
  11.9 99.4 %all-reduce.2.cloned.1.call-start = ((), (), s32[]{:S(2)}) async-start(), calls=%async_computation.3 | async-start | bytes 1572864 | tf_op jit(solution)/shard_map/psum | solution.py:187
  14.1 112.0 %reduce-scatter.2.cloned.1.call-start = ((), (), s32[]{:S(2)}) async-start(), calls=%async_computation.2 | async-start | bytes 2359296 | tf_op jit(solution)/shard_map/reduce_scatter | solution.py:167
  42.0 6.4 %copy-start.8 = (bf16[512,3072]{1,0:T(8,128)(2,1)S(1)}, bf16[512,3072]{1,0:T(8,128)(2,1)}, u32[]{:S(2)}) copy-start(bf16[512,3072]{1,0:T(8,128)(2,1)} %copy.35) | copy-start | bytes 9437188
  47.3 3.2 %copy-start.7 = (f32[256,8,128]{0,2,1:T(8,128)}, f32[256,8,128]{0,2,1:T(8,128)S(1)}, u32[]{:S(2)}) copy-start(f32[256,8,128]{0,2,1:T(8,128)S(1)} %fusion.26) | copy-start | bytes 3145732
  47.3 2.2 %copy-start.1 = (bf16[256,3072]{1,0:T(8,128)(2,1)S(1)}, bf16[256,3072]{1,0:T(8,128)(2,1)}, u32[]{:S(2)}) copy-start(bf16[256,3072]{1,0:T(8,128)(2,1)} %all-gather.2.cloned.1.call-done) | copy-start | bytes 4718596
  50.5 1.0 copy-start.9
  55.0 2.7 %copy-start.10 = (f32[256,4,128]{0,2,1:T(8,128)S(1)}, f32[256,4,128]{0,2,1:T(8,128)}, u32[]{:S(2)}) copy-start(f32[256,4,128]{0,2,1:T(8,128)} %copy-done.9) | copy-start | bytes 1572868
  55.0 2.7 %copy-start.14 = (f32[256,4,64]{0,2,1:T(8,128)S(1)}, f32[256,4,64]{0,2,1:T(8,128)}, u32[]{:S(2)}) copy-start(f32[256,4,64]{0,2,1:T(8,128)} %get-tuple-element.43) | copy-start | bytes 786436
  55.0 2.7 %copy-start.15 = (f32[256,4,64]{0,2,1:T(8,128)S(1)}, f32[256,4,64]{0,2,1:T(8,128)}, u32[]{:S(2)}) copy-start(f32[256,4,64]{0,2,1:T(8,128)} %get-tuple-element.44) | copy-start | bytes 786436
  55.0 3.5 %copy-start.11 = (bf16[1,256,1024]{1,2,0:T(8,128)(2,1)S(1)}, bf16[1,256,1024]{1,2,0:T(8,128)(2,1)}, u32[]{:S(2)}) copy-start(bf16[1,256,1024]{1,2,0:T(8,128)(2,1)} %copy.41) | copy-start | bytes 1572868
  55.0 3.5 %copy-start.16 = (bf16[256,4,128]{2,1,0:T(4,128)(2,1)S(1)}, bf16[256,4,128]{2,1,0:T(4,128)(2,1)}, u32[]{:S(2)}) copy-start(bf16[256,4,128]{2,1,0:T(4,128)(2,1)} %reshape.115) | copy-start | bytes 786436
  74.2 2.3 %copy-start.17 = (f32[256,4,128]{0,2,1:T(8,128)S(1)}, f32[256,4,128]{0,2,1:T(8,128)}, u32[]{:S(2)}) copy-start(f32[256,4,128]{0,2,1:T(8,128)} %get-tuple-element.49) | copy-start | bytes 1572868
  74.2 2.4 %copy-start.4 = (f32[4,128,2,256]{3,1,2,0:T(8,128)S(1)}, f32[4,128,2,256]{3,1,2,0:T(8,128)}, u32[]{:S(2)}) copy-start(f32[4,128,2,256]{3,1,2,0:T(8,128)} %fusion.44) | copy-start | bytes 3145732
  74.2 3.7 %slice-start = ((s8[6291456]{0:T(1024)(128)(4,1)}), s8[4194304]{0:T(1024)(128)(4,1)S(1)}, s32[]{:S(2)}) async-start(s8[6291456]{0:T(1024)(128)(4,1)} %bitcast.139), calls=%async_computation.4 | async-start | bytes 8388608
  76.5 5.6 %copy-start.12 = (bf16[4,256,128]{1,2,0:T(8,128)(2,1)}, bf16[4,256,128]{1,2,0:T(8,128)(2,1)S(1)}, u32[]{:S(2)}) copy-start(bf16[4,256,128]{1,2,0:T(8,128)(2,1)S(1)} %fusion.33) | copy-start | bytes 786436
  76.5 2.5 %slice-start.1 = ((s8[6291456]{0:T(1024)(128)(4,1)}), s8[2097152]{0:T(1024)(128)(4,1)S(1)}, s32[]{:S(2)}) async-start(s8[6291456]{0:T(1024)(128)(4,1)} %bitcast.139), calls=%async_computation.5 | async-start | bytes 4194304
  79.0 1.9 %copy-start.18 = (f32[256,4,128]{0,2,1:T(8,128)S(1)}, f32[256,4,128]{0,2,1:T(8,128)}, u32[]{:S(2)}) copy-start(f32[256,4,128]{0,2,1:T(8,128)} %get-tuple-element.50) | copy-start | bytes 1572868
  79.0 2.1 %copy-start.3 = (bf16[1,3072,512]{2,1,0:T(8,128)(2,1)S(1)}, bf16[1,3072,512]{2,1,0:T(8,128)(2,1)}, u32[]{:S(2)}) copy-start(bf16[1,3072,512]{2,1,0:T(8,128)(2,1)} %param.12) | copy-start | bytes 9437188
  111.3 3.1 %copy-start.5 = (f32[4,128,2,256]{3,1,2,0:T(8,128)S(1)}, f32[4,128,2,256]{3,1,2,0:T(8,128)}, u32[]{:S(2)}) copy-start(f32[4,128,2,256]{3,1,2,0:T(8,128)} %fusion.44) | copy-start | bytes 3145732
  111.3 3.1 %copy-start.6 = (f32[256,8,128]{0,2,1:T(8,128)S(1)}, f32[256,8,128]{0,2,1:T(8,128)}, u32[]{:S(2)}) copy-start(f32[256,8,128]{0,2,1:T(8,128)} %get-tuple-element.36) | copy-start | bytes 3145732
  114.5 1.4 copy-start.2
  114.5 1.4 copy-start.13
  121.5 4.6 %copy-start.20 = (f32[1,3072]{1,0:T(1,128)S(1)}, f32[1,3072]{1,0:T(1,128)}, u32[]{:S(2)}) copy-start(f32[1,3072]{1,0:T(1,128)} %param.10) | copy-start | bytes 36868
Sparse Core Ops, SparseCore 0:
  12.1 29.9 all-gather.1
  84.5 26.1 reduce-scatter.1
Sparse Core Ops, SparseCore 1:
  16.4 94.9 all-reduce.1
where the time goes:
time: 148 us; the launch traced here: 147 us
  matrix products  41.3 us (28%)
  waiting for transfers between devices  38.9 us (26%)
  other arithmetic  21.3 us (14%)
  local copies, waits for them, and re-layouts  20.8 us (14%)
  between operations  15.7 us (11%)
  blocking collectives  8.76 us (6%)
    psum x1, waiting for transfers between devices, body(): mean_delta = lax.psum(delta, 'rep') / replicas  27 us
    all_gather x1, waiting for transfers between devices, body(): normalized = lax.all_gather(normalized_local, 'tp', axis=0, tiled=True)  11.8 us
    psum x1, blocking collectives, body(): lax.psum(jnp.sum(summed_rows * normalized_input, axis=0), 'tp')  8.76 us
    dot_general x1, local copies, waits for them, and re-layouts, body(): jnp.dot(normalized, weight_q, preferred_element_type=jnp.float32)  8.68 us
    dot_general x1, matrix products, one_block(): jnp.einsum('grqk,qgrd->kgd', score_low, query_block, preferred_element_ty...  5.36 us
    dot_general x1, matrix products, one_block(): jnp.einsum('grqk,kgd->qgrd', score_low, rotated_keys, preferred_element_t...  5.3 us
    dot_general x1, matrix products, body(): jnp.dot(normalized, weight_q, preferred_element_type=jnp.float32)  5.26 us
    dot_general x1, local copies, waits for them, and re-layouts, body(): jnp.dot(normalized, weight_k, preferred_element_type=jnp.float32)  4.69 us
  transfers between devices with their start and end apart: 3, of which 2 were waited for; matrix products, arithmetic and copies ran while one was open for 49% of the time, Pallas kernels for 0%

commit v1 on v0

--- a/solution.py
+++ b/solution.py
@@ -1,7 +1,14 @@
+import functools
+
 import jax
 import jax.numpy as jnp
+import numpy as np
 from jax import lax
+from jax.experimental import pallas as pl
+from jax.experimental.pallas import tpu as pltpu
 from jax.sharding import PartitionSpec as P
+
+MESH = pl.DeviceIdType.MESH
 
 HEAD_SIZE = 128
 
@@ -197,6 +204,406 @@
         new_momentum,
     )
 
+NT = (((1,), (1,)), ((), ()))
+TN = (((0,), (0,)), ((), ()))
+
+
+def dot(a, b, dims=(((1,), (0,)), ((), ()))):
+    return lax.dot_general(a, b, dims, preferred_element_type=jnp.float32)
+
+
+def ds(index, size):
+    return pl.ds(pl.multiple_of(index * size, size), size)
+
+
+def host_tables(sequence_length, width):
+    middle = width // 2
+    frequency = rope_base ** (-2.0 * np.arange(middle) / width)
+    angles = np.arange(sequence_length)[:, None] * frequency[None, :]
+    cosine, sine = np.cos(angles), np.sin(angles)
+    return (
+        jnp.asarray(np.concatenate([cosine, cosine], axis=1), jnp.float32),
+        jnp.asarray(np.concatenate([-sine, sine], axis=1), jnp.float32),
+    )
+
+
+def front_kernel(
+    n_rep,
+    chunks,
+    tile,
+    tokens_ref,
+    gain_ref,
+    wq_hbm,
+    wk_hbm,
+    wv_hbm,
+    go_ref,
+    cos_ref,
+    sin_ref,
+    local_hbm,
+    normed_ref,
+    dq_ref,
+    dk_ref,
+    dv_ref,
+    mean_ref,
+    w_ref,
+    nm_ref,
+    acc_ref,
+    q_ref,
+    k_ref,
+    v_ref,
+    pieces_ref,
+    own_mean_ref,
+    all_mean_ref,
+    w_sems,
+    ag_send,
+    ag_recv,
+    fr_send,
+    fr_recv,
+    fg_send,
+    fg_recv,
+    own_sem,
+):
+    me = lax.axis_index("tp")
+    peer = 1 - me
+    rep = lax.axis_index("rep")
+    rows, width = tokens_ref.shape
+    qw, kw = wq_hbm.shape[1], wk_hbm.shape[1]
+    total = qw + 2 * kw
+    cw = width // chunks
+    piece_rows, piece_cols = own_mean_ref.shape
+    col_blocks = width // piece_cols
+    barrier = pltpu.get_barrier_semaphore()
+    pl.semaphore_signal(barrier, inc=1, device_id={"tp": peer}, device_id_type=MESH)
+
+    def greet(j, _):
+        pl.semaphore_signal(
+            barrier, inc=1, device_id={"rep": lax.rem(rep + j, n_rep)}, device_id_type=MESH
+        )
+        return 0
+
+    lax.fori_loop(1, n_rep, greet, 0)
+    weight_copies = [
+        pltpu.make_async_copy(wq_hbm, w_ref.at[:, pl.ds(0, qw)], w_sems.at[0]),
+        pltpu.make_async_copy(wk_hbm, w_ref.at[:, pl.ds(qw, kw)], w_sems.at[1]),
+        pltpu.make_async_copy(wv_hbm, w_ref.at[:, pl.ds(qw + kw, kw)], w_sems.at[2]),
+    ]
+    for copy in weight_copies:
+        copy.start()
+
+    def piece(owner):
+        return (
+            ds(owner // col_blocks, piece_rows),
+            ds(lax.rem(owner, col_blocks), piece_cols),
+        )
+
+    own_piece = pltpu.make_async_copy(local_hbm.at[piece(rep)], pieces_ref.at[0], own_sem)
+    own_piece.start()
+
+    step = 16
+
+    def norm_rows(i, _):
+        x = tokens_ref[ds(i, step), :].astype(jnp.float32)
+        inverse = lax.rsqrt(jnp.mean(x * x, axis=-1, keepdims=True) + epsilon)
+        nm_ref[pl.ds(pl.multiple_of(me * rows + i * step, step), step), :] = (
+            x * inverse * gain_ref[...]
+        ).astype(jnp.bfloat16)
+        return 0
+
+    lax.fori_loop(0, rows // step, norm_rows, 0)
+    pl.semaphore_wait(barrier, n_rep)
+
+    def gather_copy(c):
+        part = nm_ref.at[ds(me, rows), ds(c, cw)]
+        return pltpu.make_async_remote_copy(
+            src_ref=part,
+            dst_ref=part,
+            send_sem=ag_send.at[c],
+            recv_sem=ag_recv.at[c],
+            device_id={"tp": peer},
+            device_id_type=MESH,
+        )
+
+    def scatter_copy(j):
+        target = lax.rem(rep + j, n_rep)
+        return pltpu.make_async_remote_copy(
+            src_ref=local_hbm.at[piece(target)],
+            dst_ref=pieces_ref.at[j],
+            send_sem=fr_send.at[j],
+            recv_sem=fr_recv.at[j],
+            device_id={"rep": target},
+            device_id_type=MESH,
+        )
+
+    def spread_copy(j, owner):
+        return pltpu.make_async_remote_copy(
+            src_ref=own_mean_ref,
+            dst_ref=all_mean_ref.at[piece(owner)],
+            send_sem=fg_send.at[j],
+            recv_sem=fg_recv.at[j],
+            device_id={"rep": lax.rem(rep + j, n_rep)},
+            device_id_type=MESH,
+        )
+
+    def start_all(make, low, high):
+        def one(j, _):
+            make(j).start()
+            return 0
+
+        lax.fori_loop(low, high, one, 0)
+
+    def wait_recv_all(make, low, high):
+        def one(j, _):
+            make(j).wait_recv()
+            return 0
+
+        lax.fori_loop(low, high, one, 0)
+
+    def wait_send_all(make, low, high):
+        def one(j, _):
+            make(j).wait_send()
+            return 0
+
+        lax.fori_loop(low, high, one, 0)
+
+    start_all(gather_copy, 0, chunks)
+    start_all(scatter_copy, 1, n_rep)
+
+    for copy in weight_copies:
+        copy.wait()
+
+    def own_tile(t, _):
+        acc_ref[ds(me, rows), ds(t, tile)] = dot(nm_ref[ds(me, rows), :], w_ref[:, ds(t, tile)])
+        return 0
+
+    lax.fori_loop(0, total // tile, own_tile, 0)
+    acc_ref[ds(peer, rows), :] = jnp.zeros((rows, total), jnp.float32)
+
+    own_piece.wait()
+    wait_recv_all(scatter_copy, 1, n_rep)
+    summed = pieces_ref[0].astype(jnp.float32)
+    for j in range(1, n_rep):
+        summed = summed + pieces_ref[j].astype(jnp.float32)
+    summed = summed * (1.0 / n_rep)
+    own_mean_ref[...] = summed
+    all_mean_ref[piece(rep)] = summed
+    start_all(lambda j: spread_copy(j, rep), 1, n_rep)
+
+    def arrived(c, _):
+        pltpu.make_async_remote_copy(
+            src_ref=nm_ref.at[ds(peer, rows), ds(c, cw)],
+            dst_ref=nm_ref.at[ds(peer, rows), ds(c, cw)],
+            send_sem=ag_send.at[c],
+            recv_sem=ag_recv.at[c],
+            device_id={"tp": peer},
+            device_id_type=MESH,
+        ).wait_recv()
+        part = nm_ref[ds(peer, rows), ds(c, cw)]
+
+        def one(t, _):
+            acc_ref[ds(peer, rows), ds(t, tile)] += dot(part, w_ref[ds(c, cw), ds(t, tile)])
+            return 0
+
+        lax.fori_loop(0, total // tile, one, 0)
+        return 0
+
+    lax.fori_loop(0, chunks, arrived, 0)
+
+    cosine, sine = cos_ref[...], sin_ref[...]
+
+    def rope_head(source, target, index):
+        vector = acc_ref[:, ds(source, HEAD_SIZE)]
+        target[:, ds(index, HEAD_SIZE)] = (
+            vector * cosine + pltpu.roll(vector, HEAD_SIZE // 2, 1) * sine
+        ).astype(jnp.bfloat16)
+
+    heads_q, heads_kv = qw // HEAD_SIZE, kw // HEAD_SIZE
+    for h in range(heads_q):
+        rope_head(h, q_ref, h)
+    for h in range(heads_kv):
+        rope_head(heads_q + h, k_ref, h)
+    v_ref[...] = acc_ref[:, pl.ds(qw + kw, kw)].astype(jnp.bfloat16)
+
+    sequence = 2 * rows
+    group = heads_q // heads_kv
+    scale = HEAD_SIZE ** (-0.5)
+
+    def reverse(gradient, block):
+        c = cosine[block * rows : (block + 1) * rows]
+        s = sine[block * rows : (block + 1) * rows]
+        return (gradient * c - pltpu.roll(gradient, HEAD_SIZE // 2, 1) * s).astype(jnp.bfloat16)
+
+    def kv_head(g, _):
+        grad_k = [None, None]
+        grad_v = [None, None]
+        for r in range(group):
+            head = ds(g * group + r, HEAD_SIZE)
+            for b in range(2):
+                keys = (b + 1) * rows
+                block = pl.ds(b * rows, rows)
+                query = q_ref[block, head]
+                out_grad = go_ref[block, head]
+                key = k_ref[pl.ds(0, keys), ds(g, HEAD_SIZE)]
+                value = v_ref[pl.ds(0, keys), ds(g, HEAD_SIZE)]
+                scores = dot(query, key, NT) * scale
+                row = lax.broadcasted_iota(jnp.int32, scores.shape, 0) + b * rows
+                col = lax.broadcasted_iota(jnp.int32, scores.shape, 1)
+                scores = jnp.where(col <= row, scores, -jnp.inf)
+                powers = jnp.exp(scores - jnp.max(scores, axis=-1, keepdims=True))
+                prob = powers * (1.0 / jnp.sum(powers, axis=-1, keepdims=True))
+                grad_prob = dot(out_grad, value, NT)
+                inner = jnp.sum(grad_prob * prob, axis=-1, keepdims=True)
+                score_low = (prob * (grad_prob - inner) * scale).astype(jnp.bfloat16)
+                dq_ref[block, head] = reverse(dot(score_low, key), b)
+                part_v = dot(prob.astype(jnp.bfloat16), out_grad, TN)
+                part_k = dot(score_low, query, TN)
+                for j in range(b + 1):
+                    pv = part_v[j * rows : (j + 1) * rows]
+                    pk = part_k[j * rows : (j + 1) * rows]
+                    grad_v[j] = pv if grad_v[j] is None else grad_v[j] + pv
+                    grad_k[j] = pk if grad_k[j] is None else grad_k[j] + pk
+        for j in range(2):
+            block = pl.ds(j * rows, rows)
+            dk_ref[block, ds(g, HEAD_SIZE)] = reverse(grad_k[j], j)
+            dv_ref[block, ds(g, HEAD_SIZE)] = grad_v[j].astype(jnp.bfloat16)
+        return 0
+
+    lax.fori_loop(0, heads_kv, kv_head, 0)
+
+    normed_ref[...] = nm_ref[...]
+    wait_recv_all(lambda j: spread_copy(j, lax.rem(rep + n_rep - j, n_rep)), 1, n_rep)
+    mean_ref[...] = all_mean_ref[...]
+    wait_send_all(gather_copy, 0, chunks)
+    wait_send_all(scatter_copy, 1, n_rep)
+    wait_send_all(lambda j: spread_copy(j, rep), 1, n_rep)
+
+
+def pair_body(
+    n_rep,
+    tokens,
+    norm_gain,
+    w_query,
+    key_weight,
+    value_weight,
+    attention_gradient,
+    global_fragment,
+    momentum,
+    local_fragment,
+):
+    rows, width = tokens.shape[1:]
+    sequence = 2 * rows
+    weight_q, weight_k, weight_v = w_query[0], key_weight[0], value_weight[0]
+    qw, kw = weight_q.shape[1], weight_k.shape[1]
+    total = qw + 2 * kw
+    frag_rows = local_fragment.shape[1]
+    piece_rows = 16
+    piece_cols = width * frag_rows // piece_rows // n_rep
+    chunks = 6
+    bf16, f32 = jnp.bfloat16, jnp.float32
+    cosine, sine = host_tables(sequence, HEAD_SIZE)
+    vmem = pl.BlockSpec(memory_space=pltpu.VMEM)
+    anyspace = pl.BlockSpec(memory_space=pl.ANY)
+    normed, dq, dk, dv, mean_local = pl.pallas_call(
+        functools.partial(front_kernel, n_rep, chunks, 512),
+        out_shape=(
+            jax.ShapeDtypeStruct((sequence, width), bf16),
+            jax.ShapeDtypeStruct((sequence, qw), bf16),
+            jax.ShapeDtypeStruct((sequence, kw), bf16),
+            jax.ShapeDtypeStruct((sequence, kw), bf16),
+            jax.ShapeDtypeStruct((frag_rows, width), f32),
+        ),
+        in_specs=[vmem, vmem, anyspace, anyspace, anyspace, vmem, vmem, vmem, anyspace],
+        out_specs=(vmem,) * 5,
+        scratch_shapes=[
+            pltpu.VMEM((width, total), bf16),
+            pltpu.VMEM((sequence, width), bf16),
+            pltpu.VMEM((sequence, total), f32),
+            pltpu.VMEM((sequence, qw), bf16),
+            pltpu.VMEM((sequence, kw), bf16),
+            pltpu.VMEM((sequence, kw), bf16),
+            pltpu.VMEM((n_rep, piece_rows, piece_cols), bf16),
+            pltpu.VMEM((piece_rows, piece_cols), f32),
+            pltpu.VMEM((frag_rows, width), f32),
+            pltpu.SemaphoreType.DMA((3,)),
+            pltpu.SemaphoreType.DMA((chunks,)),
+            pltpu.SemaphoreType.DMA((chunks,)),
+            pltpu.SemaphoreType.DMA((n_rep,)),
+            pltpu.SemaphoreType.DMA((n_rep,)),
+            pltpu.SemaphoreType.DMA((n_rep,)),
+            pltpu.SemaphoreType.DMA((n_rep,)),
+            pltpu.SemaphoreType.DMA,
+        ],
+        compiler_params=pltpu.CompilerParams(
+            collective_id=0, has_side_effects=True, vmem_limit_bytes=40 * 1024 * 1024
+        ),
+    )(
+        tokens[0],
+        norm_gain,
+        weight_q,
+        weight_k,
+        weight_v,
+        attention_gradient[0],
+        cosine,
+        sine,
+        local_fragment[0],
+    )
+    me = lax.axis_index("tp")
+    swap = [(0, 1), (1, 0)]
+
+    def half(array, which):
+        return lax.dynamic_slice_in_dim(array, which * rows, rows, 0)
+
+    def share(which, low, high):
+        partial_value = dot(half(dq, which), weight_q[low:high], NT)
+        partial_value = partial_value + dot(half(dk, which), weight_k[low:high], NT)
+        partial_value = partial_value + dot(half(dv, which), weight_v[low:high], NT)
+        return partial_value.astype(bf16)
+
+    cuts = 2
+    step = width // cuts
+    away = [share(1 - me, c * step, (c + 1) * step) for c in range(cuts)]
+    landed = [lax.ppermute(piece, "tp", swap) for piece in away]
+    here = share(me, 0, width)
+    far = jnp.concatenate(away, axis=1)
+    gain_partial = (
+        jnp.sum(
+            far.astype(f32) * half(normed, 1 - me).astype(f32)
+            + here.astype(f32) * half(normed, me).astype(f32),
+            axis=0,
+            keepdims=True,
+        )
+        / norm_gain
+    )
+    gains_gradient = gain_partial + lax.ppermute(gain_partial, "tp", swap)
+    grad_wq = dot(normed, dq, TN).astype(bf16)
+    grad_wk = dot(normed, dk, TN).astype(bf16)
+    grad_wv = dot(normed, dv, TN).astype(bf16)
+    mean_delta = global_fragment - mean_local
+    new_momentum = outer_momentum * momentum + mean_delta
+    new_global = global_fragment - outer_rate * (mean_delta + outer_momentum * new_momentum)
+    summed_rows = here.astype(f32) + jnp.concatenate(landed, axis=1).astype(f32)
+    widened_rows = tokens[0].astype(f32)
+    inverse_norm = lax.rsqrt(
+        jnp.mean(widened_rows * widened_rows, axis=-1, keepdims=True) + epsilon
+    )
+    normalized_input = widened_rows * inverse_norm
+    scaled_rows = summed_rows * norm_gain
+    gradient_rows = (
+        inverse_norm
+        * (
+            scaled_rows
+            - normalized_input * jnp.mean(scaled_rows * normalized_input, axis=-1, keepdims=True)
+        )
+    ).astype(bf16)
+    return (
+        grad_wq[None],
+        grad_wk[None],
+        grad_wv[None],
+        gains_gradient,
+        gradient_rows[None],
+        new_global,
+        new_momentum,
+    )
+
 
 def solution(mesh):
     placed = (
@@ -210,8 +617,10 @@
         P("tp", None),
         P("rep", "tp", None),
     )
+    paired = mesh.shape["tp"] == 2
+    chosen = functools.partial(pair_body, mesh.shape["rep"]) if paired else body
     return jax.shard_map(
-        body,
+        chosen,
         mesh=mesh,
         in_specs=placed,
         out_specs=(

time: 148 us -> 82.2 us (0.56)
  waiting for transfers between devices: 38.9 us -> 0.66 us
  Pallas kernels: 0 us -> 36 us
  other arithmetic: 21.3 us -> 4.81 us
  matrix products: 41.3 us -> 25.5 us
  between operations: 15.7 us -> 0.82 us
  local copies, waits for them, and re-layouts: 20.8 us -> 11.2 us
  blocking collectives: 8.76 us -> 0 us
  starting transfers between devices: 0.12 us -> 2.6 us
    pallas_call x0 -> x1, Pallas kernels: none -> 36 us  [pair_body(): pl.pallas_call(functools.partial(front_kernel, n_rep, chunks, 512), out_s...]
    psum x1 -> x0, waiting for transfers between devices: 27 us -> none  [body(): mean_delta = lax.psum(delta, 'rep') / replicas]
    dot_general x2 -> x0, local copies, waits for them, and re-layouts: 13.4 us -> none  [the longest x1 8.68 us: body(): jnp.dot(normalized, weight_q, preferred_element_type=jnp.float32)]
    dot_general x13 -> x12, matrix products: 38.1 us -> 25.5 us  [dot(): return lax.dot_general(a, b, dims, preferred_element_type=jnp.float32)]
    all_gather x1 -> x0, waiting for transfers between devices: 11.8 us -> none  [body(): normalized = lax.all_gather(normalized_local, 'tp', axis=0, tiled=True)]
    psum x1 -> x0, blocking collectives: 8.76 us -> none  [body(): lax.psum(jnp.sum(summed_rows * normalized_input, axis=0), 'tp')]
    unnamed x46 -> x34, local copies, waits for them, and re-layouts: 3.6 us -> 11.2 us
    convert_element_type x6 -> x0, other arithmetic: 7.16 us -> none  [the longest x1 2.66 us: body(): rotate(query_rows, cosine_table, sine_table).astype(jnp.bfloat16)]
  transfers between devices with their start and end apart: 3 -> 3, of which waited for: 2 -> 1; matrix products, arithmetic and copies ran while one was open for 49% -> 29% of each run, Pallas kernels for 0% -> 0%
where the time goes in v1:
time: 82.2 us; the launch traced here: 81.7 us
  Pallas kernels  36 us (44%)
  matrix products  25.5 us (31%)
  local copies, waits for them, and re-layouts  11.2 us (14%)
  other arithmetic  4.81 us (6%)
  starting transfers between devices  2.6 us (3%)
    pallas_call x1, Pallas kernels, pair_body(): pl.pallas_call(functools.partial(front_kernel, n_rep, chunks, 512), out_s...  36 us
    dot_general x12, matrix products, dot(): return lax.dot_general(a, b, dims, preferred_element_type=jnp.float32)  25.5 us
    unnamed x34, local copies, waits for them, and re-layouts  11.2 us
    broadcast_in_dim x1, other arithmetic, pair_body(): gradient_rows[None]  2.53 us
    ppermute x2, starting transfers between devices, pair_body(): landed = [lax.ppermute(piece, 'tp', swap) for piece in away]  2.03 us
  transfers between devices with their start and end apart: 3, of which 1 were waited for; matrix products, arithmetic and copies ran while one was open for 29% of the time, Pallas kernels for 0%

profile of v1, /device:TPU:0, one launch (start us, length us, event | category | flops | bytes accessed | tf_op | source)
XLA Modules:
  0.0 81.7 jit_solution(13407773457854130350)
XLA Ops:
  0.6 0.0 copy-start
  0.7 1.9 %copy-done = bf16[1,3072,512]{2,1,0:T(8,128)(2,1)S(1)} copy-done((bf16[1,3072,512]{2,1,0:T(8,128)(2,1)S(1)}, bf16[1,3072,512]{2,1,0:T(8,128)(2,1)}, u32[]{:S(2)}) %copy-start) | copy-done | bytes 3145752
  2.5 0.0 copy-start.2
  2.5 1.9 %copy-done.2 = bf16[1,3072,512]{2,1,0:T(8,128)(2,1)S(1)} copy-done((bf16[1,3072,512]{2,1,0:T(8,128)(2,1)S(1)}, bf16[1,3072,512]{2,1,0:T(8,128)(2,1)}, u32[]{:S(2)}) %copy-start.2) | copy-done | bytes 3145752
  4.4 0.0 copy-start.4
  4.4 1.1 %copy-done.4 = bf16[1,128,3072]{2,1,0:T(8,128)(2,1)S(1)} copy-done((bf16[1,128,3072]{2,1,0:T(8,128)(2,1)S(1)}, bf16[1,128,3072]{2,1,0:T(8,128)(2,1)}, u32[]{:S(2)}) %copy-start.4) | copy-done | bytes 786456
  5.6 0.0 copy-start.8
  5.6 1.0 %copy-done.8 = bf16[1,256,1024]{2,1,0:T(8,128)(2,1)S(1)} copy-done((bf16[1,256,1024]{2,1,0:T(8,128)(2,1)S(1)}, bf16[1,256,1024]{2,1,0:T(8,128)(2,1)}, u32[]{:S(2)}) %copy-start.8) | copy-done | bytes 524312
  6.6 0.0 copy-start.9
  6.6 1.0 %copy-done.9 = bf16[1,64,3072]{2,1,0:T(8,128)(2,1)S(1)} copy-done((bf16[1,64,3072]{2,1,0:T(8,128)(2,1)S(1)}, bf16[1,64,3072]{2,1,0:T(8,128)(2,1)}, u32[]{:S(2)}) %copy-start.9) | copy-done | bytes 393240
  7.6 0.7 copy-done.10
  8.3 0.9 %copy-done.12 = f32[256,128]{1,0:T(8,128)S(1)} copy-done((f32[256,128]{1,0:T(8,128)S(1)}, f32[256,128]{1,0:T(8,128)}, u32[]{:S(2)}) %copy-start.12) | copy-done | bytes 131096
  9.2 0.9 %copy-done.13 = f32[256,128]{1,0:T(8,128)S(1)} copy-done((f32[256,128]{1,0:T(8,128)S(1)}, f32[256,128]{1,0:T(8,128)}, u32[]{:S(2)}) %copy-start.13) | copy-done | bytes 131096
  10.1 36.0 %shard_map.162 = (bf16[256,3072]{1,0:T(8,128)(2,1)S(1)}, bf16[256,1024]{1,0:T(8,128)(2,1)S(1)}, bf16[256,512]{1,0:T(8,128)(2,1)S(1)}, bf16[256,512]{1,0:T(8,128)(2,1)S(1)}, f32[64,3072]{1,0:T(8,128)S(1)}) custom-call(bf16[128,3072]{1,0:T(8,128)(2,1)S(1)} %bitcast.57, f32[1,3072]{1,0:T(1,128)S(1)} %copy-done.10, bf16[3072,1024]{1,0:T(8,128)(2,1)} %bitcast.62, ...), custom_call_target="tpu_custom_call" | custom-call | tf_op jit(solution)/shard_map/pallas_call | solution.py:505
  46.1 0.0 copy-start.6
  46.2 0.6 fusion.29
  46.8 0.0 copy-done.14
  46.8 1.2 %fusion.10 = f32[128,1536]{1,0:T(8,128)S(1)} fusion(f32[128,1536]{1,0:T(8,128)S(1)} %fusion.29, bf16[1,3072,1024]{2,1,0:T(8,128)(2,1)S(1)} %copy-done.14, bf16[256,1024]{1,0:T(8,128)(2,1)S(1)} %get-tuple-element.13, s32[]{:T(128)S(6)} %select_n.4), kind=kOutput, calls=%fused_computation.15 | convolution fusion | flops 402849792 | bytes 4980740 | tf_op jit(solution)/shard_map/dot_general | solution.py:212
  48.0 0.0 copy-done.6
  48.0 1.4 %fusion.16 = bf16[128,1536]{1,0:T(8,128)(2,1)} fusion(f32[128,1536]{1,0:T(8,128)S(1)} %fusion.10, bf16[1,3072,512]{2,1,0:T(8,128)(2,1)S(1)} %copy-done.2, bf16[256,512]{1,0:T(8,128)(2,1)S(1)} %get-tuple-element.15, s32[]{:T(128)S(6)} %select_n.4), kind=kOutput, calls=%fused_computation.19 | convolution fusion | flops 201719808 | bytes 2883588 | tf_op jit(solution)/shard_map/dot_general | solution.py:212
  49.4 0.5 collective-permute-start.1
  49.9 0.6 fusion.26
  50.6 1.2 %fusion.13 = f32[128,1536]{1,0:T(8,128)S(1)} fusion(f32[128,1536]{1,0:T(8,128)S(1)} %fusion.26, bf16[1,3072,1024]{2,1,0:T(8,128)(2,1)S(1)} %copy-done.14, bf16[256,1024]{1,0:T(8,128)(2,1)S(1)} %get-tuple-element.13, s32[]{:T(128)S(6)} %select_n.4), kind=kOutput, calls=%fused_computation.16 | convolution fusion | flops 402849792 | bytes 4980740 | tf_op jit(solution)/shard_map/dot_general | solution.py:212
  51.8 0.0 copy-start.5
  51.8 1.4 %fusion.17 = bf16[128,1536]{1,0:T(8,128)(2,1)} fusion(f32[128,1536]{1,0:T(8,128)S(1)} %fusion.13, bf16[1,3072,512]{2,1,0:T(8,128)(2,1)S(1)} %copy-done.2, bf16[256,512]{1,0:T(8,128)(2,1)S(1)} %get-tuple-element.15, s32[]{:T(128)S(6)} %select_n.4), kind=kOutput, calls=%fused_computation.20 | convolution fusion | flops 201719808 | bytes 2883588 | tf_op jit(solution)/shard_map/dot_general | solution.py:212
  53.2 1.5 %collective-permute-start.2 = (bf16[128,1536]{1,0:T(8,128)(2,1)}, bf16[128,1536]{1,0:T(8,128)(2,1)}, u32[]{:S(2)}, u32[]{:S(2)}) collective-permute-start(bf16[128,1536]{1,0:T(8,128)(2,1)} %fusion.17), channel_id=1, source_target_pairs={{0,1},{1,0},{2,3},{3,2},{4,5},{5,4},{6,7},{7,6},{8,9},{9,8},{10,11... | collective-permute-start | bytes 1179656 | tf_op jit(solution)/shard_map/ppermute | solution.py:564
  54.7 0.0 copy-done.5
  54.7 0.2 fusion.24
  55.0 2.7 %fusion = bf16[1,3072,512]{2,1,0:T(8,128)(2,1)} fusion(bf16[256,3072]{1,0:T(8,128)(2,1)S(1)} %get-tuple-element.12, bf16[256,512]{1,0:T(8,128)(2,1)S(1)} %get-tuple-element.14), kind=kOutput, calls=%fused_computation.3 | convolution fusion | flops 806879232 | bytes 4980736 | tf_op jit(solution)/shard_map/dot_general | solution.py:212
  57.7 2.7 %fusion.1 = bf16[1,3072,512]{2,1,0:T(8,128)(2,1)} fusion(bf16[256,3072]{1,0:T(8,128)(2,1)S(1)} %get-tuple-element.12, bf16[256,512]{1,0:T(8,128)(2,1)S(1)} %get-tuple-element.15), kind=kOutput, calls=%fused_computation.4 | convolution fusion | flops 806879232 | bytes 4980736 | tf_op jit(solution)/shard_map/dot_general | solution.py:212
  60.3 4.5 %convert_bitcast_fusion = bf16[1,3072,1024]{2,1,0:T(8,128)(2,1)} fusion(bf16[256,3072]{1,0:T(8,128)(2,1)S(1)} %get-tuple-element.12, bf16[256,1024]{1,0:T(8,128)(2,1)S(1)} %get-tuple-element.13), kind=kOutput, calls=%fused_computation | convolution fusion | flops 1613758464 | bytes 8388608 | tf_op jit(solution)/shard_map/dot_general | solution.py:212
  64.9 5.1 %fusion.36 = f32[128,3072]{1,0:T(8,128)S(1)} fusion(bf16[256,1024]{1,0:T(8,128)(2,1)S(1)} %get-tuple-element.13, s32[]{:T(128)S(6)} %select_n.5, bf16[1,3072,1024]{2,1,0:T(8,128)(2,1)} %param.13), kind=kOutput, calls=%fused_computation.46 | convolution fusion | flops 805306368 | bytes 8126468 | tf_op jit(solution)/shard_map/dot_general | solution.py:212
  70.0 0.0 copy-done.7
  70.0 0.0 copy-done.15
  70.0 0.0 copy-done.16
  70.0 0.0 copy-start.1
  70.0 1.4 %multiply_subtract_fusion = (f32[64,3072]{1,0:T(8,128)}, f32[64,3072]{1,0:T(8,128)}) fusion(f32[64,3072]{1,0:T(8,128)S(1)} %copy-done.15, f32[64,3072]{1,0:T(8,128)S(1)} %copy-done.16, f32[64,3072]{1,0:T(8,128)S(1)} %copy-done.7), kind=kLoop, calls=%fused_computation.44 | loop fusion | flops 1376256 | bytes 3932160 | tf_op jit(solution)/shard_map/sub | solution.py:582
  71.4 1.1 %copy-done.1 = bf16[1,3072,512]{2,1,0:T(8,128)(2,1)S(1)} copy-done((bf16[1,3072,512]{2,1,0:T(8,128)(2,1)S(1)}, bf16[1,3072,512]{2,1,0:T(8,128)(2,1)}, u32[]{:S(2)}) %copy-start.1) | copy-done | bytes 3145752
  72.5 1.2 %convolution_add_fusion.1 = f32[128,3072]{1,0:T(8,128)S(1)} fusion(f32[128,3072]{1,0:T(8,128)S(1)} %fusion.36, bf16[256,512]{1,0:T(8,128)(2,1)S(1)} %get-tuple-element.14, s32[]{:T(128)S(6)} %select_n.5, bf16[1,3072,512]{2,1,0:T(8,128)(2,1)S(1)} %copy-done.1), kind=kOutput, calls=%fused_computation.6 | convolution fusion | flops 403046400 | bytes 6422532 | tf_op jit(solution)/shard_map/dot_general | solution.py:212
  73.7 0.0 collective-permute-done.1
  73.7 0.0 collective-permute-done.2
  73.7 0.7 copy-done.3
  74.4 0.0 copy-done.11
  74.4 2.9 %fusion.20 = (f32[128]{0:T(128)S(1)}, f32[3072]{0:T(1024)S(1)}, f32[128,3072]{1,0:T(8,128)S(1)}) fusion(f32[3072]{0:T(1024)S(1)} %bitcast.60, f32[128]{0:T(128)S(1)} %add_rsqrt_fusion, bf16[128,1536]{1,0:T(8,128)(2,1)} %collective-permute-done.2, bf16[128,1536]{1,0:T(8,128)(2,1)} %collective-permute-done.1, bf16[1,128,3072]{2,1,0:T(8,128)(2,1)S(1)} %copy-done.5, ...), kind=kOutput, calls=%fused_computation.25 | convolution fusion | flops 411693952 | bytes 10381824 | tf_op jit(solution)/shard_map/dot_general | solution.py:212
  77.3 0.6 collective-permute-start
  77.9 2.5 %fusion.35 = bf16[1,128,3072]{2,1,0:T(8,128)(2,1)} fusion(f32[128,3072]{1,0:T(8,128)S(1)} %get-tuple-element.21, f32[128]{0:T(128)S(1)} %broadcast_multiply_fusion, f32[3072]{0:T(1024)S(1)} %bitcast.61, f32[128]{0:T(128)S(1)} %add_rsqrt_fusion, bf16[128,1536]{1,0:T(8,128)(2,1)} %collective-permute-done.2, bf16[128,1536]{1,0:T(8,128)(2,1)} %collective-permute-done.1, ...), kind=kLoop, calls=%fused_computation.42 | loop fusion | flops 4718592 | bytes 3945472 | tf_op jit(solution)/shard_map/broadcast_in_dim | solution.py:602
  80.4 0.7 collective-permute-done
  81.1 0.6 add.68
  (12 shorter events, 0.0 us)
Async XLA Ops:
  0.6 1.9 %copy-start = (bf16[1,3072,512]{2,1,0:T(8,128)(2,1)S(1)}, bf16[1,3072,512]{2,1,0:T(8,128)(2,1)}, u32[]{:S(2)}) copy-start(bf16[1,3072,512]{2,1,0:T(8,128)(2,1)} %param.14) | copy-start | bytes 9437188
  2.5 1.9 %copy-start.2 = (bf16[1,3072,512]{2,1,0:T(8,128)(2,1)S(1)}, bf16[1,3072,512]{2,1,0:T(8,128)(2,1)}, u32[]{:S(2)}) copy-start(bf16[1,3072,512]{2,1,0:T(8,128)(2,1)} %param.15) | copy-start | bytes 9437188
  4.4 1.1 %copy-start.4 = (bf16[1,128,3072]{2,1,0:T(8,128)(2,1)S(1)}, bf16[1,128,3072]{2,1,0:T(8,128)(2,1)}, u32[]{:S(2)}) copy-start(bf16[1,128,3072]{2,1,0:T(8,128)(2,1)} %param.11) | copy-start | bytes 2359300
  5.6 1.0 %copy-start.8 = (bf16[1,256,1024]{2,1,0:T(8,128)(2,1)S(1)}, bf16[1,256,1024]{2,1,0:T(8,128)(2,1)}, u32[]{:S(2)}) copy-start(bf16[1,256,1024]{2,1,0:T(8,128)(2,1)} %param.16) | copy-start | bytes 1572868
  6.6 1.0 %copy-start.9 = (bf16[1,64,3072]{2,1,0:T(8,128)(2,1)S(1)}, bf16[1,64,3072]{2,1,0:T(8,128)(2,1)}, u32[]{:S(2)}) copy-start(bf16[1,64,3072]{2,1,0:T(8,128)(2,1)} %param.19) | copy-start | bytes 1179652
  7.6 0.7 copy-start.10
  8.3 0.9 %copy-start.12 = (f32[256,128]{1,0:T(8,128)S(1)}, f32[256,128]{1,0:T(8,128)}, u32[]{:S(2)}) copy-start(f32[256,128]{1,0:T(8,128)} %constant.28.clone.cos_ref) | copy-start | bytes 393220
  9.2 0.9 %copy-start.13 = (f32[256,128]{1,0:T(8,128)S(1)}, f32[256,128]{1,0:T(8,128)}, u32[]{:S(2)}) copy-start(f32[256,128]{1,0:T(8,128)} %constant.29.clone.sin_ref) | copy-start | bytes 393220
  10.1 36.7 %copy-start.14 = (bf16[1,3072,1024]{2,1,0:T(8,128)(2,1)S(1)}, bf16[1,3072,1024]{2,1,0:T(8,128)(2,1)}, u32[]{:S(2)}) copy-start(bf16[1,3072,1024]{2,1,0:T(8,128)(2,1)} %param.13) | copy-start | bytes 18874372
  46.1 1.9 %copy-start.6 = (f32[64,3072]{1,0:T(8,128)}, f32[64,3072]{1,0:T(8,128)S(1)}, u32[]{:S(2)}) copy-start(f32[64,3072]{1,0:T(8,128)S(1)} %get-tuple-element.16) | copy-start | bytes 2359300
  49.4 24.2 %collective-permute-start.1 = (bf16[128,1536]{1,0:T(8,128)(2,1)}, bf16[128,1536]{1,0:T(8,128)(2,1)}, u32[]{:S(2)}, u32[]{:S(2)}) collective-permute-start(bf16[128,1536]{1,0:T(8,128)(2,1)} %fusion.16), channel_id=1, source_target_pairs={{0,1},{1,0},{2,3},{3,2},{4,5},{5,4},{6,7},{7,6},{8,9},{9,8},{10,11... | collective-permute-start | bytes 1179656 | tf_op jit(solution)/shard_map/ppermute | solution.py:564
  51.8 2.9 %copy-start.5 = (bf16[1,128,3072]{2,1,0:T(8,128)(2,1)S(1)}, bf16[1,128,3072]{2,1,0:T(8,128)(2,1)}, u32[]{:S(2)}) copy-start(bf16[1,128,3072]{2,1,0:T(8,128)(2,1)} %param.11) | copy-start | bytes 2359300
  53.2 20.5 %collective-permute-start.2 = (bf16[128,1536]{1,0:T(8,128)(2,1)}, bf16[128,1536]{1,0:T(8,128)(2,1)}, u32[]{:S(2)}, u32[]{:S(2)}) collective-permute-start(bf16[128,1536]{1,0:T(8,128)(2,1)} %fusion.17), channel_id=1, source_target_pairs={{0,1},{1,0},{2,3},{3,2},{4,5},{5,4},{6,7},{7,6},{8,9},{9,8},{10,11... | collective-permute-start | bytes 1179656 | tf_op jit(solution)/shard_map/ppermute | solution.py:564
  64.9 5.1 %copy-start.7 = (f32[64,3072]{1,0:T(8,128)S(1)}, f32[64,3072]{1,0:T(8,128)}, u32[]{:S(2)}) copy-start(f32[64,3072]{1,0:T(8,128)} %copy-done.6) | copy-start | bytes 2359300
  64.9 5.1 %copy-start.15 = (f32[64,3072]{1,0:T(8,128)S(1)}, f32[64,3072]{1,0:T(8,128)}, u32[]{:S(2)}) copy-start(f32[64,3072]{1,0:T(8,128)} %param.17) | copy-start | bytes 2359300
  64.9 5.1 %copy-start.16 = (f32[64,3072]{1,0:T(8,128)S(1)}, f32[64,3072]{1,0:T(8,128)}, u32[]{:S(2)}) copy-start(f32[64,3072]{1,0:T(8,128)} %param.18) | copy-start | bytes 2359300
  70.0 2.5 %copy-start.1 = (bf16[1,3072,512]{2,1,0:T(8,128)(2,1)S(1)}, bf16[1,3072,512]{2,1,0:T(8,128)(2,1)}, u32[]{:S(2)}) copy-start(bf16[1,3072,512]{2,1,0:T(8,128)(2,1)} %param.14) | copy-start | bytes 9437188
  72.5 1.9 %copy-start.3 = (bf16[1,3072,512]{2,1,0:T(8,128)(2,1)S(1)}, bf16[1,3072,512]{2,1,0:T(8,128)(2,1)}, u32[]{:S(2)}) copy-start(bf16[1,3072,512]{2,1,0:T(8,128)(2,1)} %param.15) | copy-start | bytes 9437188
  72.5 1.9 %copy-start.11 = (f32[1,3072]{1,0:T(1,128)S(1)}, f32[1,3072]{1,0:T(1,128)}, u32[]{:S(2)}) copy-start(f32[1,3072]{1,0:T(1,128)} %gain_ref.1) | copy-start | bytes 36868
  77.3 3.8 %collective-permute-start = (f32[1,3072]{1,0:T(1,128)S(1)}, f32[1,3072]{1,0:T(1,128)S(1)}, u32[]{:S(2)}, u32[]{:S(2)}) collective-permute-start(f32[1,3072]{1,0:T(1,128)S(1)} %div.9), channel_id=1, source_target_pairs={{0,1},{1,0},{2,3},{3,2},{4,5},{5,4},{6,7},{7,6},{8,9},{9,8},{10,11... | collective-permute-start | bytes 36872 | tf_op jit(solution)/shard_map/ppermute | solution.py:576

commit v2 on v1

--- a/solution.py
+++ b/solution.py
@@ -231,29 +231,38 @@
     n_rep,
     chunks,
     tile,
-    tokens_ref,
-    gain_ref,
+    tokens_hbm,
+    gain_hbm,
     wq_hbm,
     wk_hbm,
     wv_hbm,
+    go_hbm,
+    cos_hbm,
+    sin_hbm,
+    local_hbm,
+    normed_hbm,
+    grads_hbm,
+    away_hbm,
+    mean_hbm,
+    tokens_ref,
+    gain_ref,
     go_ref,
     cos_ref,
     sin_ref,
-    local_hbm,
-    normed_ref,
-    dq_ref,
-    dk_ref,
-    dv_ref,
-    mean_ref,
     w_ref,
     nm_ref,
     acc_ref,
     q_ref,
     k_ref,
     v_ref,
+    grads_ref,
+    away_ref,
     pieces_ref,
     own_mean_ref,
     all_mean_ref,
+    in_sems,
+    out_sems,
+    away_sems,
     w_sems,
     ag_send,
     ag_recv,
@@ -272,6 +281,20 @@
     cw = width // chunks
     piece_rows, piece_cols = own_mean_ref.shape
     col_blocks = width // piece_cols
+    loads = [
+        pltpu.make_async_copy(source, target, in_sems.at[i])
+        for i, (source, target) in enumerate(
+            (
+                (tokens_hbm, tokens_ref),
+                (gain_hbm, gain_ref),
+                (cos_hbm, cos_ref),
+                (sin_hbm, sin_ref),
+                (go_hbm, go_ref),
+            )
+        )
+    ]
+    for copy in loads:
+        copy.start()
     barrier = pltpu.get_barrier_semaphore()
     pl.semaphore_signal(barrier, inc=1, device_id={"tp": peer}, device_id_type=MESH)
 
@@ -299,6 +322,8 @@
     own_piece = pltpu.make_async_copy(local_hbm.at[piece(rep)], pieces_ref.at[0], own_sem)
     own_piece.start()
 
+    for copy in loads:
+        copy.wait()
     step = 16
 
     def norm_rows(i, _):
@@ -408,6 +433,8 @@
 
     lax.fori_loop(0, chunks, arrived, 0)
 
+    normed_out = pltpu.make_async_copy(nm_ref, normed_hbm, out_sems.at[0])
+    normed_out.start()
     cosine, sine = cos_ref[...], sin_ref[...]
 
     def rope_head(source, target, index):
@@ -453,7 +480,7 @@
                 grad_prob = dot(out_grad, value, NT)
                 inner = jnp.sum(grad_prob * prob, axis=-1, keepdims=True)
                 score_low = (prob * (grad_prob - inner) * scale).astype(jnp.bfloat16)
-                dq_ref[block, head] = reverse(dot(score_low, key), b)
+                grads_ref[block, head] = reverse(dot(score_low, key), b)
                 part_v = dot(prob.astype(jnp.bfloat16), out_grad, TN)
                 part_k = dot(score_low, query, TN)
                 for j in range(b + 1):
@@ -463,18 +490,96 @@
                     grad_k[j] = pk if grad_k[j] is None else grad_k[j] + pk
         for j in range(2):
             block = pl.ds(j * rows, rows)
-            dk_ref[block, ds(g, HEAD_SIZE)] = reverse(grad_k[j], j)
-            dv_ref[block, ds(g, HEAD_SIZE)] = grad_v[j].astype(jnp.bfloat16)
+            grads_ref[block, ds(heads_q + g, HEAD_SIZE)] = reverse(grad_k[j], j)
+            grads_ref[block, ds(heads_q + heads_kv + g, HEAD_SIZE)] = grad_v[j].astype(jnp.bfloat16)
         return 0
 
     lax.fori_loop(0, heads_kv, kv_head, 0)
 
-    normed_ref[...] = nm_ref[...]
+    grads_out = pltpu.make_async_copy(grads_ref, grads_hbm, out_sems.at[1])
+    grads_out.start()
     wait_recv_all(lambda j: spread_copy(j, lax.rem(rep + n_rep - j, n_rep)), 1, n_rep)
-    mean_ref[...] = all_mean_ref[...]
+    mean_out = pltpu.make_async_copy(all_mean_ref, mean_hbm, out_sems.at[2])
+    mean_out.start()
+
+    def away_copy(c):
+        columns = ds(c, cw)
+        return pltpu.make_async_copy(
+            away_ref.at[:, columns], away_hbm.at[:, columns], away_sems.at[c]
+        )
+
+    def share(c, _):
+        away_ref[:, ds(c, cw)] = dot(
+            grads_ref[ds(peer, rows), :], w_ref[ds(c, cw), :], NT
+        ).astype(jnp.bfloat16)
+        away_copy(c).start()
+        return 0
+
+    lax.fori_loop(0, chunks, share, 0)
     wait_send_all(gather_copy, 0, chunks)
     wait_send_all(scatter_copy, 1, n_rep)
     wait_send_all(lambda j: spread_copy(j, rep), 1, n_rep)
+    normed_out.wait()
+    grads_out.wait()
+    mean_out.wait()
+    for c in range(chunks):
+        away_copy(c).wait()
+
+
+def weight_kernel(
+    rows,
+    normed_ref,
+    grads_ref,
+    away_ref,
+    gain_ref,
+    wq_ref,
+    wk_ref,
+    wv_ref,
+    global_ref,
+    momentum_ref,
+    mean_ref,
+    dwq_ref,
+    dwk_ref,
+    dwv_ref,
+    here_ref,
+    gain_out,
+    new_global,
+    new_momentum,
+):
+    me = lax.axis_index("tp")
+    qw, kw = wq_ref.shape[1], wk_ref.shape[1]
+    own = ds(me, rows)
+    here = dot(grads_ref[own, pl.ds(0, qw)], wq_ref[...], NT)
+    here = here + dot(grads_ref[own, pl.ds(qw, kw)], wk_ref[...], NT)
+    here = here + dot(grads_ref[own, pl.ds(qw + kw, kw)], wv_ref[...], NT)
+    here = here.astype(jnp.bfloat16)
+    here_ref[...] = here
+    normed = normed_ref[...]
+    dwq_ref[...] = dot(normed, grads_ref[:, pl.ds(0, qw)], TN).astype(jnp.bfloat16)
+    dwk_ref[...] = dot(normed, grads_ref[:, pl.ds(qw, kw)], TN).astype(jnp.bfloat16)
+    dwv_ref[...] = dot(normed, grads_ref[:, pl.ds(qw + kw, kw)], TN).astype(jnp.bfloat16)
+    products = here.astype(jnp.float32) * normed_ref[own, :].astype(jnp.float32)
+    products += away_ref[...].astype(jnp.float32) * normed_ref[ds(1 - me, rows), :].astype(
+        jnp.float32
+    )
+    gain_out[...] = jnp.sum(products, axis=0, keepdims=True) / gain_ref[...]
+    outer = global_ref[...]
+    mean_delta = outer - mean_ref[...]
+    updated = outer_momentum * momentum_ref[...] + mean_delta
+    new_momentum[...] = updated
+    new_global[...] = outer - outer_rate * (mean_delta + outer_momentum * updated)
+
+
+def tail_kernel(tokens_ref, gain_ref, here_ref, landed_ref, mine_ref, other_ref, out_ref, total_ref):
+    x = tokens_ref[...].astype(jnp.float32)
+    inverse = lax.rsqrt(jnp.mean(x * x, axis=-1, keepdims=True) + epsilon)
+    xhat = x * inverse
+    band = tokens_ref.shape[0]
+    landed = landed_ref[ds(pl.program_id(0), band), :].astype(jnp.float32)
+    scaled = (here_ref[...].astype(jnp.float32) + landed) * gain_ref[...]
+    inner = jnp.mean(scaled * xhat, axis=-1, keepdims=True)
+    out_ref[...] = (inverse * (scaled - xhat * inner)).astype(jnp.bfloat16)
+    total_ref[...] = mine_ref[...] + other_ref[...]
 
 
 def pair_body(
@@ -502,27 +607,36 @@
     cosine, sine = host_tables(sequence, HEAD_SIZE)
     vmem = pl.BlockSpec(memory_space=pltpu.VMEM)
     anyspace = pl.BlockSpec(memory_space=pl.ANY)
-    normed, dq, dk, dv, mean_local = pl.pallas_call(
+    normed, grads, away, mean_local = pl.pallas_call(
         functools.partial(front_kernel, n_rep, chunks, 512),
         out_shape=(
             jax.ShapeDtypeStruct((sequence, width), bf16),
-            jax.ShapeDtypeStruct((sequence, qw), bf16),
-            jax.ShapeDtypeStruct((sequence, kw), bf16),
-            jax.ShapeDtypeStruct((sequence, kw), bf16),
+            jax.ShapeDtypeStruct((sequence, total), bf16),
+            jax.ShapeDtypeStruct((rows, width), bf16),
             jax.ShapeDtypeStruct((frag_rows, width), f32),
         ),
-        in_specs=[vmem, vmem, anyspace, anyspace, anyspace, vmem, vmem, vmem, anyspace],
-        out_specs=(vmem,) * 5,
+        in_specs=[anyspace] * 9,
+        out_specs=(anyspace,) * 4,
         scratch_shapes=[
+            pltpu.VMEM((rows, width), bf16),
+            pltpu.VMEM((1, width), f32),
+            pltpu.VMEM((sequence, qw), bf16),
+            pltpu.VMEM((sequence, HEAD_SIZE), f32),
+            pltpu.VMEM((sequence, HEAD_SIZE), f32),
             pltpu.VMEM((width, total), bf16),
             pltpu.VMEM((sequence, width), bf16),
             pltpu.VMEM((sequence, total), f32),
             pltpu.VMEM((sequence, qw), bf16),
             pltpu.VMEM((sequence, kw), bf16),
             pltpu.VMEM((sequence, kw), bf16),
+            pltpu.VMEM((sequence, total), bf16),
+            pltpu.VMEM((rows, width), bf16),
             pltpu.VMEM((n_rep, piece_rows, piece_cols), bf16),
             pltpu.VMEM((piece_rows, piece_cols), f32),
             pltpu.VMEM((frag_rows, width), f32),
+            pltpu.SemaphoreType.DMA((5,)),
+            pltpu.SemaphoreType.DMA((3,)),
+            pltpu.SemaphoreType.DMA((chunks,)),
             pltpu.SemaphoreType.DMA((3,)),
             pltpu.SemaphoreType.DMA((chunks,)),
             pltpu.SemaphoreType.DMA((chunks,)),
@@ -533,7 +647,7 @@
             pltpu.SemaphoreType.DMA,
         ],
         compiler_params=pltpu.CompilerParams(
-            collective_id=0, has_side_effects=True, vmem_limit_bytes=40 * 1024 * 1024
+            collective_id=0, has_side_effects=True, vmem_limit_bytes=60 * 1024 * 1024
         ),
     )(
         tokens[0],
@@ -546,54 +660,85 @@
         sine,
         local_fragment[0],
     )
-    me = lax.axis_index("tp")
     swap = [(0, 1), (1, 0)]
-
-    def half(array, which):
-        return lax.dynamic_slice_in_dim(array, which * rows, rows, 0)
-
-    def share(which, low, high):
-        partial_value = dot(half(dq, which), weight_q[low:high], NT)
-        partial_value = partial_value + dot(half(dk, which), weight_k[low:high], NT)
-        partial_value = partial_value + dot(half(dv, which), weight_v[low:high], NT)
-        return partial_value.astype(bf16)
-
-    cuts = 2
-    step = width // cuts
-    away = [share(1 - me, c * step, (c + 1) * step) for c in range(cuts)]
-    landed = [lax.ppermute(piece, "tp", swap) for piece in away]
-    here = share(me, 0, width)
-    far = jnp.concatenate(away, axis=1)
-    gain_partial = (
-        jnp.sum(
-            far.astype(f32) * half(normed, 1 - me).astype(f32)
-            + here.astype(f32) * half(normed, me).astype(f32),
-            axis=0,
-            keepdims=True,
-        )
-        / norm_gain
-    )
-    gains_gradient = gain_partial + lax.ppermute(gain_partial, "tp", swap)
-    grad_wq = dot(normed, dq, TN).astype(bf16)
-    grad_wk = dot(normed, dk, TN).astype(bf16)
-    grad_wv = dot(normed, dv, TN).astype(bf16)
-    mean_delta = global_fragment - mean_local
-    new_momentum = outer_momentum * momentum + mean_delta
-    new_global = global_fragment - outer_rate * (mean_delta + outer_momentum * new_momentum)
-    summed_rows = here.astype(f32) + jnp.concatenate(landed, axis=1).astype(f32)
-    widened_rows = tokens[0].astype(f32)
-    inverse_norm = lax.rsqrt(
-        jnp.mean(widened_rows * widened_rows, axis=-1, keepdims=True) + epsilon
-    )
-    normalized_input = widened_rows * inverse_norm
-    scaled_rows = summed_rows * norm_gain
-    gradient_rows = (
-        inverse_norm
-        * (
-            scaled_rows
-            - normalized_input * jnp.mean(scaled_rows * normalized_input, axis=-1, keepdims=True)
-        )
-    ).astype(bf16)
+    landed = lax.ppermute(away, "tp", swap)
+    cw = width // chunks
+
+    def columns(height):
+        return pl.BlockSpec((height, cw), lambda i: (0, i))
+
+    def rows_of(breadth):
+        return pl.BlockSpec((cw, breadth), lambda i: (i, 0))
+
+    grad_wq, grad_wk, grad_wv, here, gain_partial, new_global, new_momentum = pl.pallas_call(
+        functools.partial(weight_kernel, rows),
+        grid=(chunks,),
+        out_shape=(
+            jax.ShapeDtypeStruct((width, qw), bf16),
+            jax.ShapeDtypeStruct((width, kw), bf16),
+            jax.ShapeDtypeStruct((width, kw), bf16),
+            jax.ShapeDtypeStruct((rows, width), bf16),
+            jax.ShapeDtypeStruct((1, width), f32),
+            jax.ShapeDtypeStruct((frag_rows, width), f32),
+            jax.ShapeDtypeStruct((frag_rows, width), f32),
+        ),
+        in_specs=[
+            columns(sequence),
+            pl.BlockSpec((sequence, total), lambda i: (0, 0)),
+            columns(rows),
+            columns(1),
+            rows_of(qw),
+            rows_of(kw),
+            rows_of(kw),
+            columns(frag_rows),
+            columns(frag_rows),
+            columns(frag_rows),
+        ],
+        out_specs=(
+            rows_of(qw),
+            rows_of(kw),
+            rows_of(kw),
+            columns(rows),
+            columns(1),
+            columns(frag_rows),
+            columns(frag_rows),
+        ),
+        compiler_params=pltpu.CompilerParams(vmem_limit_bytes=60 * 1024 * 1024),
+        cost_estimate=pl.CostEstimate(
+            flops=6 * sequence * width * total // 2,
+            bytes_accessed=4 * width * total + 12 * frag_rows * width * 2,
+            transcendentals=0,
+        ),
+    )(
+        normed,
+        grads,
+        away,
+        norm_gain,
+        weight_q,
+        weight_k,
+        weight_v,
+        global_fragment,
+        momentum,
+        mean_local,
+    )
+    gain_other = lax.ppermute(gain_partial, "tp", swap)
+    band = 32
+    row_block = pl.BlockSpec((band, width), lambda i: (i, 0))
+    whole_row = pl.BlockSpec((1, width), lambda i: (0, 0))
+    gradient_rows, gains_gradient = pl.pallas_call(
+        tail_kernel,
+        grid=(rows // band,),
+        out_shape=(
+            jax.ShapeDtypeStruct((rows, width), bf16),
+            jax.ShapeDtypeStruct((1, width), f32),
+        ),
+        in_specs=[row_block, whole_row, row_block, vmem, vmem, vmem],
+        out_specs=(row_block, whole_row),
+        compiler_params=pltpu.CompilerParams(vmem_limit_bytes=16 * 1024 * 1024),
+        cost_estimate=pl.CostEstimate(
+            flops=10 * rows * width, bytes_accessed=8 * rows * width, transcendentals=0
+        ),
+    )(tokens[0], norm_gain, here, landed, gain_partial, gain_other)
     return (
         grad_wq[None],
         grad_wk[None],

time: 82.2 us -> 67.5 us (0.82)
  matrix products: 25.5 us -> 0 us
  Pallas kernels: 36 us -> 60.1 us
  local copies, waits for them, and re-layouts: 11.2 us -> 1.84 us
  other arithmetic: 4.81 us -> 0 us
  waiting for transfers between devices: 0.66 us -> 2.39 us
    dot_general x12 -> x0, matrix products: 25.5 us -> none  [dot(): return lax.dot_general(a, b, dims, preferred_element_type=jnp.float32)]
    pallas_call x0 -> x2, Pallas kernels: none -> 18.7 us  [the longest x1 16.5 us: pair_body(): pl.pallas_call(functools.partial(weight_kernel, rows), grid=(chunks,), ou...]
    unnamed x34 -> x8, local copies, waits for them, and re-layouts: 11.2 us -> 1.84 us
    pallas_call x1, Pallas kernels: 36 us -> 41.4 us  [pair_body(): pl.pallas_call(functools.partial(front_kernel, n_rep, chunks, 512), out_s...]
    broadcast_in_dim x1 -> x0, other arithmetic: 2.53 us -> none  [pair_body(): gradient_rows[None]]
    ppermute x3 -> x2, waiting for transfers between devices: 0.66 us -> 2.39 us  [the longest x1 2.38 us: pair_body(): gain_other = lax.ppermute(gain_partial, 'tp', swap)]
    sub x1 -> x0, other arithmetic: 1.39 us -> none  [pair_body(): global_fragment - outer_rate * (mean_delta + outer_momentum * new_momentum)]
    ppermute x3 -> x2, starting transfers between devices: 2.6 us -> 2.16 us  [the longest x1 1.59 us: pair_body(): gain_other = lax.ppermute(gain_partial, 'tp', swap)]
  transfers between devices with their start and end apart: 3 -> 2, of which waited for: 1 -> 1; matrix products, arithmetic and copies ran while one was open for 29% -> 0% of each run, Pallas kernels for 0% -> 25%
where the time goes in v2:
time: 67.5 us; the launch traced here: 67.2 us
  Pallas kernels  60.1 us (89%)
  waiting for transfers between devices  2.39 us (4%)
  starting transfers between devices  2.16 us (3%)
  local copies, waits for them, and re-layouts  1.84 us (3%)
    pallas_call x1, Pallas kernels, pair_body(): pl.pallas_call(functools.partial(front_kernel, n_rep, chunks, 512), out_s...  41.4 us
    pallas_call x1, Pallas kernels, pair_body(): pl.pallas_call(functools.partial(weight_kernel, rows), grid=(chunks,), ou...  16.5 us
    ppermute x1, waiting for transfers between devices, pair_body(): gain_other = lax.ppermute(gain_partial, 'tp', swap)  2.38 us
    pallas_call x1, Pallas kernels, pair_body(): pl.pallas_call(tail_kernel, grid=(rows // band,), out_shape=(jax.ShapeDty...  2.2 us
    unnamed x8, local copies, waits for them, and re-layouts  1.84 us
    ppermute x1, starting transfers between devices, pair_body(): gain_other = lax.ppermute(gain_partial, 'tp', swap)  1.59 us
  transfers between devices with their start and end apart: 2, of which 1 were waited for; matrix products, arithmetic and copies ran while one was open for 0% of the time, Pallas kernels for 25%

profile of v2, /device:TPU:0, one launch (start us, length us, event | category | flops | bytes accessed | tf_op | source)
XLA Modules:
  0.0 67.2 jit_solution(13573444180854606945)
XLA Ops:
  0.6 41.4 %shard_map.162 = (bf16[256,3072]{1,0:T(8,128)(2,1)}, bf16[256,2048]{1,0:T(8,128)(2,1)}, bf16[128,3072]{1,0:T(8,128)(2,1)}, f32[64,3072]{1,0:T(8,128)}) custom-call(bf16[128,3072]{1,0:T(8,128)(2,1)} %bitcast.10, f32[1,3072]{1,0:T(1,128)} %gain_ref.3, bf16[3072,1024]{1,0:T(8,128)(2,1)} %bitcast.12, bf16[3072,512]{1,0:T(8,128)(2,1)} %bitcast.14, ...), custom_call_target="tpu_custom_call" | custom-call | tf_op jit(solution)/shard_map/pallas_call | solution.py:610
  42.1 0.6 collective-permute-start
  42.6 0.0 copy-start
  42.6 0.0 copy-start.2
  42.6 16.5 %shard_map.163 = (bf16[3072,1024]{1,0:T(8,128)(2,1)}, bf16[3072,512]{1,0:T(8,128)(2,1)}, bf16[3072,512]{1,0:T(8,128)(2,1)}, bf16[128,3072]{1,0:T(8,128)(2,1)}, f...) custom-call(bf16[256,3072]{1,0:T(8,128)(2,1)} %get-tuple-element.20.normed_ref, ...), custom_call_target="tpu_custom_call" | custom-call | flops 4831838208 | bytes 29884416 | tf_op jit(solution)/shard_map/pallas_call | solution.py:673
  59.2 1.6 %collective-permute-start.1 = (f32[1,3072]{1,0:T(1,128)}, f32[1,3072]{1,0:T(1,128)S(1)}, u32[]{:S(2)}, u32[]{:S(2)}) collective-permute-start(f32[1,3072]{1,0:T(1,128)} %get-tuple-element.28.mine_ref), channel_id=1, source_target_pairs={{0,1},{1,0},{2,3},{3,2},{4,5},{5,4},{6,7},{7,6},{8,9},{9,8},{10,11... | collective-permute-start | bytes 36872 | tf_op jit(solution)/shard_map/ppermute | solution.py:724
  60.8 2.4 %collective-permute-done.1.other_ref = f32[1,3072]{1,0:T(1,128)S(1)} collective-permute-done((f32[1,3072]{1,0:T(1,128)}, f32[1,3072]{1,0:T(1,128)S(1)}, u32[]{:S(2)}, u32[]{:S(2)}) %collective-permute-start.1) | collective-permute-done | bytes 12320 | tf_op jit(solution)/shard_map/ppermute | solution.py:724
  63.1 0.0 collective-permute-done.landed_ref
  63.1 0.0 copy-done
  63.1 0.0 copy-done.2
  63.1 0.0 copy-start.1
  63.2 1.1 %copy-done.1 = bf16[128,3072]{1,0:T(8,128)(2,1)S(1)} copy-done((bf16[128,3072]{1,0:T(8,128)(2,1)S(1)}, bf16[128,3072]{1,0:T(8,128)(2,1)}, u32[]{:S(2)}) %copy-start.1) | copy-done | bytes 786456
  64.3 0.0 copy-start.3
  64.3 0.7 %copy-done.3 = f32[1,3072]{1,0:T(1,128)S(1)} copy-done((f32[1,3072]{1,0:T(1,128)S(1)}, f32[1,3072]{1,0:T(1,128)}, u32[]{:S(2)}) %copy-start.3) | copy-done | bytes 12312
  65.0 2.2 %shard_map.164 = (bf16[128,3072]{1,0:T(8,128)(2,1)}, f32[1,3072]{1,0:T(1,128)}) custom-call(bf16[128,3072]{1,0:T(8,128)(2,1)S(1)} %bitcast.11, f32[1,3072]{1,0:T(1,128)S(1)} %copy-done.2, bf16[128,3072]{1,0:T(8,128)(2,1)S(1)} %copy-done.1, bf16[128,3072]{1,0:T(8,128)(2,1)S(1)} %collective-permute-done.landed_ref, f32[1,3072]{1,0:T(1,128)S(1)} %copy-done.3, ...), custom_call_target="tpu_custom_call" | custom-call | flops 3932160 | bytes 3145728 | tf_op jit(solution)/shard_map/pallas_call | solution.py:728
Async XLA Ops:
  42.1 21.1 %collective-permute-start = (bf16[128,3072]{1,0:T(8,128)(2,1)}, bf16[128,3072]{1,0:T(8,128)(2,1)S(1)}, u32[]{:S(2)}, u32[]{:S(2)}) collective-permute-start(bf16[128,3072]{1,0:T(8,128)(2,1)} %get-tuple-element.22.away_ref), channel_id=1, source_target_pairs={{0,1},{1,0},{2,3},{3,2},{4,5},{5,4},{6,7},{7,6},{8,9},{9,8},{10,11... | collective-permute-start | bytes 2359304 | tf_op jit(solution)/shard_map/ppermute | solution.py:664
  42.6 20.5 %copy-start = (bf16[1,128,3072]{2,1,0:T(8,128)(2,1)S(1)}, bf16[1,128,3072]{2,1,0:T(8,128)(2,1)}, u32[]{:S(2)}) copy-start(bf16[1,128,3072]{2,1,0:T(8,128)(2,1)} %param.11) | copy-start | bytes 2359300
  42.6 20.5 %copy-start.2 = (f32[1,3072]{1,0:T(1,128)S(1)}, f32[1,3072]{1,0:T(1,128)}, u32[]{:S(2)}) copy-start(f32[1,3072]{1,0:T(1,128)} %gain_ref.3) | copy-start | bytes 36868
  59.2 4.0 %collective-permute-start.1 = (f32[1,3072]{1,0:T(1,128)}, f32[1,3072]{1,0:T(1,128)S(1)}, u32[]{:S(2)}, u32[]{:S(2)}) collective-permute-start(f32[1,3072]{1,0:T(1,128)} %get-tuple-element.28.mine_ref), channel_id=1, source_target_pairs={{0,1},{1,0},{2,3},{3,2},{4,5},{5,4},{6,7},{7,6},{8,9},{9,8},{10,11... | collective-permute-start | bytes 36872 | tf_op jit(solution)/shard_map/ppermute | solution.py:724
  63.1 1.1 %copy-start.1 = (bf16[128,3072]{1,0:T(8,128)(2,1)S(1)}, bf16[128,3072]{1,0:T(8,128)(2,1)}, u32[]{:S(2)}) copy-start(bf16[128,3072]{1,0:T(8,128)(2,1)} %get-tuple-element.27.here_ref) | copy-start | bytes 2359300
  64.3 0.7 %copy-start.3 = (f32[1,3072]{1,0:T(1,128)S(1)}, f32[1,3072]{1,0:T(1,128)}, u32[]{:S(2)}) copy-start(f32[1,3072]{1,0:T(1,128)} %get-tuple-element.28.mine_ref) | copy-start | bytes 36868

commit v3 on v2

--- a/solution.py
+++ b/solution.py
@@ -240,9 +240,11 @@
     cos_hbm,
     sin_hbm,
     local_hbm,
+    outer_hbm,
     normed_hbm,
     grads_hbm,
     away_hbm,
+    here_hbm,
     mean_hbm,
     tokens_ref,
     gain_ref,
@@ -256,13 +258,15 @@
     k_ref,
     v_ref,
     grads_ref,
-    away_ref,
+    shares_ref,
     pieces_ref,
     own_mean_ref,
     all_mean_ref,
+    outer_ref,
     in_sems,
     out_sems,
     away_sems,
+    here_sems,
     w_sems,
     ag_send,
     ag_recv,
@@ -319,8 +323,10 @@
             ds(lax.rem(owner, col_blocks), piece_cols),
         )
 
-    own_piece = pltpu.make_async_copy(local_hbm.at[piece(rep)], pieces_ref.at[0], own_sem)
+    own_piece = pltpu.make_async_copy(local_hbm.at[piece(rep)], pieces_ref.at[0], own_sem.at[0])
     own_piece.start()
+    own_outer = pltpu.make_async_copy(outer_hbm.at[piece(rep)], outer_ref, own_sem.at[1])
+    own_outer.start()
 
     for copy in loads:
         copy.wait()
@@ -404,11 +410,12 @@
     acc_ref[ds(peer, rows), :] = jnp.zeros((rows, total), jnp.float32)
 
     own_piece.wait()
+    own_outer.wait()
     wait_recv_all(scatter_copy, 1, n_rep)
     summed = pieces_ref[0].astype(jnp.float32)
     for j in range(1, n_rep):
         summed = summed + pieces_ref[j].astype(jnp.float32)
-    summed = summed * (1.0 / n_rep)
+    summed = (outer_ref[...] - summed * (1.0 / n_rep)).astype(jnp.bfloat16)
     own_mean_ref[...] = summed
     all_mean_ref[piece(rep)] = summed
     start_all(lambda j: spread_copy(j, rep), 1, n_rep)
@@ -498,24 +505,31 @@
 
     grads_out = pltpu.make_async_copy(grads_ref, grads_hbm, out_sems.at[1])
     grads_out.start()
+
+    def away_copy(c):
+        columns = ds(c, cw)
+        return pltpu.make_async_copy(
+            shares_ref.at[ds(peer, rows), columns], away_hbm.at[:, columns], away_sems.at[c]
+        )
+
+    def here_copy(c):
+        columns = ds(c, cw)
+        return pltpu.make_async_copy(
+            shares_ref.at[ds(me, rows), columns], here_hbm.at[:, columns], here_sems.at[c]
+        )
+
+    def share(c, _):
+        shares_ref[:, ds(c, cw)] = dot(grads_ref[...], w_ref[ds(c, cw), :], NT).astype(
+            jnp.bfloat16
+        )
+        away_copy(c).start()
+        here_copy(c).start()
+        return 0
+
+    lax.fori_loop(0, chunks, share, 0)
     wait_recv_all(lambda j: spread_copy(j, lax.rem(rep + n_rep - j, n_rep)), 1, n_rep)
     mean_out = pltpu.make_async_copy(all_mean_ref, mean_hbm, out_sems.at[2])
     mean_out.start()
-
-    def away_copy(c):
-        columns = ds(c, cw)
-        return pltpu.make_async_copy(
-            away_ref.at[:, columns], away_hbm.at[:, columns], away_sems.at[c]
-        )
-
-    def share(c, _):
-        away_ref[:, ds(c, cw)] = dot(
-            grads_ref[ds(peer, rows), :], w_ref[ds(c, cw), :], NT
-        ).astype(jnp.bfloat16)
-        away_copy(c).start()
-        return 0
-
-    lax.fori_loop(0, chunks, share, 0)
     wait_send_all(gather_copy, 0, chunks)
     wait_send_all(scatter_copy, 1, n_rep)
     wait_send_all(lambda j: spread_copy(j, rep), 1, n_rep)
@@ -524,6 +538,7 @@
     mean_out.wait()
     for c in range(chunks):
         away_copy(c).wait()
+        here_copy(c).wait()
 
 
 def weight_kernel(
@@ -531,40 +546,33 @@
     normed_ref,
     grads_ref,
     away_ref,
+    here_ref,
     gain_ref,
-    wq_ref,
-    wk_ref,
-    wv_ref,
+    momentum_ref,
     global_ref,
-    momentum_ref,
     mean_ref,
     dwq_ref,
     dwk_ref,
     dwv_ref,
-    here_ref,
     gain_out,
     new_global,
     new_momentum,
 ):
     me = lax.axis_index("tp")
-    qw, kw = wq_ref.shape[1], wk_ref.shape[1]
+    qw, kw = dwq_ref.shape[1], dwk_ref.shape[1]
     own = ds(me, rows)
-    here = dot(grads_ref[own, pl.ds(0, qw)], wq_ref[...], NT)
-    here = here + dot(grads_ref[own, pl.ds(qw, kw)], wk_ref[...], NT)
-    here = here + dot(grads_ref[own, pl.ds(qw + kw, kw)], wv_ref[...], NT)
-    here = here.astype(jnp.bfloat16)
-    here_ref[...] = here
-    normed = normed_ref[...]
-    dwq_ref[...] = dot(normed, grads_ref[:, pl.ds(0, qw)], TN).astype(jnp.bfloat16)
-    dwk_ref[...] = dot(normed, grads_ref[:, pl.ds(qw, kw)], TN).astype(jnp.bfloat16)
-    dwv_ref[...] = dot(normed, grads_ref[:, pl.ds(qw + kw, kw)], TN).astype(jnp.bfloat16)
-    products = here.astype(jnp.float32) * normed_ref[own, :].astype(jnp.float32)
+    columns = ds(pl.program_id(0), normed_ref.shape[1])
+    turned = normed_ref[...].T
+    dwq_ref[...] = dot(turned, grads_ref[:, pl.ds(0, qw)]).astype(jnp.bfloat16)
+    dwk_ref[...] = dot(turned, grads_ref[:, pl.ds(qw, kw)]).astype(jnp.bfloat16)
+    dwv_ref[...] = dot(turned, grads_ref[:, pl.ds(qw + kw, kw)]).astype(jnp.bfloat16)
+    products = here_ref[...].astype(jnp.float32) * normed_ref[own, :].astype(jnp.float32)
     products += away_ref[...].astype(jnp.float32) * normed_ref[ds(1 - me, rows), :].astype(
         jnp.float32
     )
-    gain_out[...] = jnp.sum(products, axis=0, keepdims=True) / gain_ref[...]
+    gain_out[:, columns] = jnp.sum(products, axis=0, keepdims=True) / gain_ref[...]
     outer = global_ref[...]
-    mean_delta = outer - mean_ref[...]
+    mean_delta = mean_ref[...].astype(jnp.float32)
     updated = outer_momentum * momentum_ref[...] + mean_delta
     new_momentum[...] = updated
     new_global[...] = outer - outer_rate * (mean_delta + outer_momentum * updated)
@@ -576,7 +584,8 @@
     xhat = x * inverse
     band = tokens_ref.shape[0]
     landed = landed_ref[ds(pl.program_id(0), band), :].astype(jnp.float32)
-    scaled = (here_ref[...].astype(jnp.float32) + landed) * gain_ref[...]
+    here = here_ref[ds(pl.program_id(0), band), :].astype(jnp.float32)
+    scaled = (here + landed) * gain_ref[...]
     inner = jnp.mean(scaled * xhat, axis=-1, keepdims=True)
     out_ref[...] = (inverse * (scaled - xhat * inner)).astype(jnp.bfloat16)
     total_ref[...] = mine_ref[...] + other_ref[...]
@@ -607,16 +616,17 @@
     cosine, sine = host_tables(sequence, HEAD_SIZE)
     vmem = pl.BlockSpec(memory_space=pltpu.VMEM)
     anyspace = pl.BlockSpec(memory_space=pl.ANY)
-    normed, grads, away, mean_local = pl.pallas_call(
+    normed, grads, away, here, mean_delta = pl.pallas_call(
         functools.partial(front_kernel, n_rep, chunks, 512),
         out_shape=(
             jax.ShapeDtypeStruct((sequence, width), bf16),
             jax.ShapeDtypeStruct((sequence, total), bf16),
             jax.ShapeDtypeStruct((rows, width), bf16),
-            jax.ShapeDtypeStruct((frag_rows, width), f32),
+            jax.ShapeDtypeStruct((rows, width), bf16),
+            jax.ShapeDtypeStruct((frag_rows, width), bf16),
         ),
-        in_specs=[anyspace] * 9,
-        out_specs=(anyspace,) * 4,
+        in_specs=[anyspace] * 10,
+        out_specs=(anyspace,) * 5,
         scratch_shapes=[
             pltpu.VMEM((rows, width), bf16),
             pltpu.VMEM((1, width), f32),
@@ -630,12 +640,14 @@
             pltpu.VMEM((sequence, kw), bf16),
             pltpu.VMEM((sequence, kw), bf16),
             pltpu.VMEM((sequence, total), bf16),
-            pltpu.VMEM((rows, width), bf16),
+            pltpu.VMEM((sequence, width), bf16),
             pltpu.VMEM((n_rep, piece_rows, piece_cols), bf16),
+            pltpu.VMEM((piece_rows, piece_cols), bf16),
+            pltpu.VMEM((frag_rows, width), bf16),
             pltpu.VMEM((piece_rows, piece_cols), f32),
-            pltpu.VMEM((frag_rows, width), f32),
             pltpu.SemaphoreType.DMA((5,)),
             pltpu.SemaphoreType.DMA((3,)),
+            pltpu.SemaphoreType.DMA((chunks,)),
             pltpu.SemaphoreType.DMA((chunks,)),
             pltpu.SemaphoreType.DMA((3,)),
             pltpu.SemaphoreType.DMA((chunks,)),
@@ -644,7 +656,7 @@
             pltpu.SemaphoreType.DMA((n_rep,)),
             pltpu.SemaphoreType.DMA((n_rep,)),
             pltpu.SemaphoreType.DMA((n_rep,)),
-            pltpu.SemaphoreType.DMA,
+            pltpu.SemaphoreType.DMA((2,)),
         ],
         compiler_params=pltpu.CompilerParams(
             collective_id=0, has_side_effects=True, vmem_limit_bytes=60 * 1024 * 1024
@@ -659,6 +671,7 @@
         cosine,
         sine,
         local_fragment[0],
+        global_fragment,
     )
     swap = [(0, 1), (1, 0)]
     landed = lax.ppermute(away, "tp", swap)
@@ -670,14 +683,13 @@
     def rows_of(breadth):
         return pl.BlockSpec((cw, breadth), lambda i: (i, 0))
 
-    grad_wq, grad_wk, grad_wv, here, gain_partial, new_global, new_momentum = pl.pallas_call(
+    grad_wq, grad_wk, grad_wv, gain_partial, new_global, new_momentum = pl.pallas_call(
         functools.partial(weight_kernel, rows),
         grid=(chunks,),
         out_shape=(
             jax.ShapeDtypeStruct((width, qw), bf16),
             jax.ShapeDtypeStruct((width, kw), bf16),
             jax.ShapeDtypeStruct((width, kw), bf16),
-            jax.ShapeDtypeStruct((rows, width), bf16),
             jax.ShapeDtypeStruct((1, width), f32),
             jax.ShapeDtypeStruct((frag_rows, width), f32),
             jax.ShapeDtypeStruct((frag_rows, width), f32),
@@ -686,10 +698,8 @@
             columns(sequence),
             pl.BlockSpec((sequence, total), lambda i: (0, 0)),
             columns(rows),
+            columns(rows),
             columns(1),
-            rows_of(qw),
-            rows_of(kw),
-            rows_of(kw),
             columns(frag_rows),
             columns(frag_rows),
             columns(frag_rows),
@@ -698,28 +708,25 @@
             rows_of(qw),
             rows_of(kw),
             rows_of(kw),
-            columns(rows),
-            columns(1),
+            vmem,
             columns(frag_rows),
             columns(frag_rows),
         ),
-        compiler_params=pltpu.CompilerParams(vmem_limit_bytes=60 * 1024 * 1024),
+        compiler_params=pltpu.CompilerParams(vmem_limit_bytes=52 * 1024 * 1024),
         cost_estimate=pl.CostEstimate(
-            flops=6 * sequence * width * total // 2,
-            bytes_accessed=4 * width * total + 12 * frag_rows * width * 2,
+            flops=2 * sequence * width * total,
+            bytes_accessed=2 * width * total + 12 * frag_rows * width * 2,
             transcendentals=0,
         ),
     )(
         normed,
         grads,
         away,
+        here,
         norm_gain,
-        weight_q,
-        weight_k,
-        weight_v,
+        momentum,
         global_fragment,
-        momentum,
-        mean_local,
+        mean_delta,
     )
     gain_other = lax.ppermute(gain_partial, "tp", swap)
     band = 32
@@ -732,7 +739,7 @@
             jax.ShapeDtypeStruct((rows, width), bf16),
             jax.ShapeDtypeStruct((1, width), f32),
         ),
-        in_specs=[row_block, whole_row, row_block, vmem, vmem, vmem],
+        in_specs=[row_block, whole_row, vmem, vmem, vmem, vmem],
         out_specs=(row_block, whole_row),
         compiler_params=pltpu.CompilerParams(vmem_limit_bytes=16 * 1024 * 1024),
         cost_estimate=pl.CostEstimate(

time: 67.5 us -> 63.9 us (0.947)
  Pallas kernels: 60.1 us -> 52.6 us
  waiting for transfers between devices: 2.39 us -> 4.82 us
  local copies, waits for them, and re-layouts: 1.84 us -> 3.27 us
    pallas_call x1, Pallas kernels: 16.5 us -> 9.36 us  [pair_body(): pl.pallas_call(functools.partial(weight_kernel, rows), grid=(chunks,), ou...]
    ppermute x1, waiting for transfers between devices: 2.38 us -> 4.82 us  [pair_body(): gain_other = lax.ppermute(gain_partial, 'tp', swap)]
    unnamed x8 -> x10, local copies, waits for them, and re-layouts: 1.84 us -> 3.27 us
  transfers between devices with their start and end apart: 2 -> 2, of which waited for: 1 -> 1; matrix products, arithmetic and copies ran while one was open for 0% -> 0% of each run, Pallas kernels for 25% -> 15%
where the time goes in v3:
time: 63.9 us; the launch traced here: 63.5 us
  Pallas kernels  52.6 us (82%)
  waiting for transfers between devices  4.82 us (8%)
  local copies, waits for them, and re-layouts  3.27 us (5%)
  starting transfers between devices  2.09 us (3%)
  between operations  0.66 us (1%)
    pallas_call x1, Pallas kernels, pair_body(): pl.pallas_call(functools.partial(front_kernel, n_rep, chunks, 512), out_s...  41 us
    pallas_call x1, Pallas kernels, pair_body(): pl.pallas_call(functools.partial(weight_kernel, rows), grid=(chunks,), ou...  9.36 us
    ppermute x1, waiting for transfers between devices, pair_body(): gain_other = lax.ppermute(gain_partial, 'tp', swap)  4.82 us
    unnamed x10, local copies, waits for them, and re-layouts  3.27 us
    pallas_call x1, Pallas kernels, pair_body(): pl.pallas_call(tail_kernel, grid=(rows // band,), out_shape=(jax.ShapeDty...  2.23 us
    ppermute x1, starting transfers between devices, pair_body(): gain_other = lax.ppermute(gain_partial, 'tp', swap)  1.52 us
  transfers between devices with their start and end apart: 2, of which 1 were waited for; matrix products, arithmetic and copies ran while one was open for 0% of the time, Pallas kernels for 15%

profile of v3, /device:TPU:0, one launch (start us, length us, event | category | flops | bytes accessed | tf_op | source)
XLA Modules:
  0.0 63.5 jit_solution(18353307300084899206)
XLA Ops:
  0.6 0.0 copy-start.2
  0.6 41.0 %shard_map.162 = (bf16[256,3072]{1,0:T(8,128)(2,1)}, bf16[256,2048]{1,0:T(8,128)(2,1)}, bf16[128,3072]{1,0:T(8,128)(2,1)}, bf16[128,3072]{1,0:T(8,128)(2,1)}, bf16[64,3072]{1,0:T(8,128)(2,1)}) custom-call(bf16[128,3072]{1,0:T(8,128)(2,1)} %bitcast.10, f32[1,3072]{1,0:T(1,128)} %gain_ref.3, bf16[3072,1024]{1,0:T(8,128)(2,1)} %bitcast.12, ...), custom_call_target="tpu_custom_call" | custom-call | tf_op jit(solution)/shard_map/pallas_call | solution.py:619
  41.7 0.6 collective-permute-start
  42.3 0.0 copy-done.2
  42.3 0.0 copy-start.1
  42.3 1.1 %copy-done.1 = bf16[128,3072]{1,0:T(8,128)(2,1)S(1)} copy-done((bf16[128,3072]{1,0:T(8,128)(2,1)S(1)}, bf16[128,3072]{1,0:T(8,128)(2,1)}, u32[]{:S(2)}) %copy-start.1) | copy-done | bytes 786456
  43.4 0.0 copy-start.3
  43.4 1.1 %copy-done.3 = bf16[128,3072]{1,0:T(8,128)(2,1)S(1)} copy-done((bf16[128,3072]{1,0:T(8,128)(2,1)S(1)}, bf16[128,3072]{1,0:T(8,128)(2,1)}, u32[]{:S(2)}) %copy-start.3) | copy-done | bytes 786456
  44.5 0.0 copy-start.4
  44.5 1.0 %copy-done.4 = bf16[64,3072]{1,0:T(8,128)(2,1)S(1)} copy-done((bf16[64,3072]{1,0:T(8,128)(2,1)S(1)}, bf16[64,3072]{1,0:T(8,128)(2,1)}, u32[]{:S(2)}) %copy-start.4) | copy-done | bytes 393240
  45.5 0.0 copy-start
  45.5 9.4 %shard_map.163 = (bf16[3072,1024]{1,0:T(8,128)(2,1)}, bf16[3072,512]{1,0:T(8,128)(2,1)}, bf16[3072,512]{1,0:T(8,128)(2,1)}, f32[1,3072]{1,0:T(1,128)S(1)}, f32[64,3072]{1,0:T(8,128)}, /*index=5*/f32[64,3072]{1,0:T(8,128)}) custom-call(bf16[256,3072]{1,0:T(8,128)(2,1)} %get-tuple-element.20.normed_ref, bf16[256,2048]{1,0:T(8,128)(2,1)} %get-tuple-element.21.grads_ref, ...), custom_call_target="tpu_custom_call" | custom-call | flops 3221225472 | bytes 17301504 | tf_op jit(solution)/shard_map/pallas_call | solution.py:686
  54.9 1.5 %collective-permute-start.1 = (f32[1,3072]{1,0:T(1,128)S(1)}, f32[1,3072]{1,0:T(1,128)S(1)}, u32[]{:S(2)}, u32[]{:S(2)}) collective-permute-start(f32[1,3072]{1,0:T(1,128)S(1)} %get-tuple-element.28.mine_ref), channel_id=1, source_target_pairs={{0,1},{1,0},{2,3},{3,2},{4,5},{5,4},{6,7},{7,6},{8,9},{9,8},{10,11... | collective-permute-start | bytes 36872 | tf_op jit(solution)/shard_map/ppermute | solution.py:731
  56.4 4.8 %collective-permute-done.1.other_ref = f32[1,3072]{1,0:T(1,128)S(1)} collective-permute-done((f32[1,3072]{1,0:T(1,128)S(1)}, f32[1,3072]{1,0:T(1,128)S(1)}, u32[]{:S(2)}, u32[]{:S(2)}) %collective-permute-start.1) | collective-permute-done | bytes 12320 | tf_op jit(solution)/shard_map/ppermute | solution.py:731
  61.2 0.0 collective-permute-done.landed_ref
  61.2 0.0 copy-done
  61.2 2.2 %shard_map.164 = (bf16[128,3072]{1,0:T(8,128)(2,1)}, f32[1,3072]{1,0:T(1,128)}) custom-call(bf16[128,3072]{1,0:T(8,128)(2,1)S(1)} %bitcast.11, f32[1,3072]{1,0:T(1,128)S(1)} %copy-done.2, bf16[128,3072]{1,0:T(8,128)(2,1)S(1)} %copy-done.1, bf16[128,3072]{1,0:T(8,128)(2,1)S(1)} %collective-permute-done.landed_ref, f32[1,3072]{1,0:T(1,128)S(1)} %get-tuple-element.28.mine_ref, ...), custom_call_target="tpu_custom_call" | custom-call | flops 3932160 | bytes 3145728 | tf_op jit(solution)/shard_map/pallas_call | solution.py:735
Async XLA Ops:
  0.6 41.6 %copy-start.2 = (f32[1,3072]{1,0:T(1,128)S(1)}, f32[1,3072]{1,0:T(1,128)}, u32[]{:S(2)}) copy-start(f32[1,3072]{1,0:T(1,128)} %gain_ref.3) | copy-start | bytes 36868
  41.7 19.5 %collective-permute-start = (bf16[128,3072]{1,0:T(8,128)(2,1)}, bf16[128,3072]{1,0:T(8,128)(2,1)S(1)}, u32[]{:S(2)}, u32[]{:S(2)}) collective-permute-start(bf16[128,3072]{1,0:T(8,128)(2,1)} %get-tuple-element.22.away_ref), channel_id=1, source_target_pairs={{0,1},{1,0},{2,3},{3,2},{4,5},{5,4},{6,7},{7,6},{8,9},{9,8},{10,11... | collective-permute-start | bytes 2359304 | tf_op jit(solution)/shard_map/ppermute | solution.py:677
  42.3 1.1 %copy-start.1 = (bf16[128,3072]{1,0:T(8,128)(2,1)S(1)}, bf16[128,3072]{1,0:T(8,128)(2,1)}, u32[]{:S(2)}) copy-start(bf16[128,3072]{1,0:T(8,128)(2,1)} %get-tuple-element.23.here_ref) | copy-start | bytes 2359300
  43.4 1.1 %copy-start.3 = (bf16[128,3072]{1,0:T(8,128)(2,1)S(1)}, bf16[128,3072]{1,0:T(8,128)(2,1)}, u32[]{:S(2)}) copy-start(bf16[128,3072]{1,0:T(8,128)(2,1)} %get-tuple-element.22.away_ref) | copy-start | bytes 2359300
  44.5 1.0 %copy-start.4 = (bf16[64,3072]{1,0:T(8,128)(2,1)S(1)}, bf16[64,3072]{1,0:T(8,128)(2,1)}, u32[]{:S(2)}) copy-start(bf16[64,3072]{1,0:T(8,128)(2,1)} %get-tuple-element.24.mean_ref) | copy-start | bytes 1179652
  45.5 15.7 %copy-start = (bf16[1,128,3072]{2,1,0:T(8,128)(2,1)S(1)}, bf16[1,128,3072]{2,1,0:T(8,128)(2,1)}, u32[]{:S(2)}) copy-start(bf16[1,128,3072]{2,1,0:T(8,128)(2,1)} %param.11) | copy-start | bytes 2359300
  54.9 6.3 %collective-permute-start.1 = (f32[1,3072]{1,0:T(1,128)S(1)}, f32[1,3072]{1,0:T(1,128)S(1)}, u32[]{:S(2)}, u32[]{:S(2)}) collective-permute-start(f32[1,3072]{1,0:T(1,128)S(1)} %get-tuple-element.28.mine_ref), channel_id=1, source_target_pairs={{0,1},{1,0},{2,3},{3,2},{4,5},{5,4},{6,7},{7,6},{8,9},{9,8},{10,11... | collective-permute-start | bytes 36872 | tf_op jit(solution)/shard_map/ppermute | solution.py:731
